TPU v7x, 32 devices: a 4x4x1 block of a 4x4x8 slice. The times are simulated.
32 devices in a mesh: batch: 1 (over z), row: 4 (over y), col: 8 (over x, core).
Axes of the slice: x: 4, y: 4, z: 1, core: 2. Of those that a mesh axis runs over, the one named last changes fastest.
The devices are a block of a 4x4x8 slice.
Arguments:
- a_mat: bfloat16 [7168, 7168], P(('batch', 'row'), 'col')
- x_start: float32 [7168, 256], P(('batch', 'row', 'col'))
- shifts: float32 [32], P('batch')
Outputs:
- output 1: float32 [7168, 256], P(('batch', 'row', 'col'))
- output 2: float32 [256, 256], P('batch')
All inputs are finite; a program needn't handle non-finite values.
Results may differ from a plain program's by a relative error of at most 0.00141845.
Values are sent between devices in bfloat16 or wider.
A program may use at most 768 MiB of HBM per device.

v0:
```python
import jax
import jax.numpy as jnp
from jax import lax
from jax.sharding import PartitionSpec as P

FULL_PRECISION = lax.Precision.HIGHEST
ROW_CONTRACT = (((0,), (0,)), ((), ()))
GRID_AXES = ("row", "col")


def orthonormalize(y_loc, total_rows):
    y_low = y_loc.astype(jnp.bfloat16)
    gram_one = lax.psum(lax.dot_general(y_low, y_low, ROW_CONTRACT, preferred_element_type=jnp.float32), GRID_AXES) / total_rows
    chol_one = jnp.linalg.cholesky(gram_one)
    y_mid = lax.linalg.triangular_solve(chol_one, y_loc, left_side=False, lower=True, transpose_a=True)
    gram_two = lax.psum(lax.dot_general(y_mid, y_mid, ROW_CONTRACT, precision=FULL_PRECISION, preferred_element_type=jnp.float32), GRID_AXES) / total_rows
    chol_two = jnp.linalg.cholesky(gram_two)
    return lax.linalg.triangular_solve(chol_two, y_mid, left_side=False, lower=True, transpose_a=True)


def solution(mesh):
    row_count = mesh.shape["row"]
    col_count = mesh.shape["col"]
    perm_pairs = [(col_idx * row_count + row_idx, row_idx * col_count + col_idx) for row_idx in range(row_count) for col_idx in range(col_count)]

    def apply_operator(a_blk, x_loc):
        x_low = x_loc.astype(jnp.bfloat16)
        x_moved = lax.ppermute(x_low, GRID_AXES, perm_pairs)
        x_column = lax.all_gather(x_moved, "row", axis=0, tiled=True)
        partial_rows = jnp.dot(a_blk, x_column, preferred_element_type=jnp.float32)
        return lax.psum_scatter(partial_rows, "col", scatter_dimension=0, tiled=True)

    def local_program(a_blk, x_loc, shift_vec):
        total_rows = a_blk.shape[0] * row_count
        for sweep_idx in range(shift_vec.shape[0]):
            applied = apply_operator(a_blk, x_loc)
            x_loc = orthonormalize(applied - shift_vec[sweep_idx] * x_loc, total_rows)
        applied = apply_operator(a_blk, x_loc)
        local_part = lax.dot_general(x_loc, applied, ROW_CONTRACT, precision=FULL_PRECISION, preferred_element_type=jnp.float32)
        rayleigh = lax.psum(local_part, GRID_AXES) / total_rows
        return x_loc, rayleigh

    return jax.shard_map(
        local_program,
        mesh=mesh,
        in_specs=(P(("batch", "row"), "col"), P(("batch", "row", "col"), None), P("batch")),
        out_specs=(P(("batch", "row", "col"), None), P("batch", None)),
        check_vma=False,
    )
```

profile of v0, /device:TPU:97, one launch (start us, length us, event | category | flops | bytes accessed | tf_op | source)
XLA Modules:
  0.0 13485.5 jit_solution(11725301952066318235)
XLA Ops:
  68.9 95.3 all-reduce.67.cloned.1.call-done
  250.3 92.2 all-reduce.69.cloned.1.call-done
  484.1 95.4 all-reduce.71.cloned.1.call-done
  666.8 92.1 all-reduce.73.cloned.1.call-done
  899.8 95.5 all-reduce.75.cloned.1.call-done
  1082.7 92.1 all-reduce.77.cloned.1.call-done
  1315.6 95.7 all-reduce.79.cloned.1.call-done
  1498.7 92.1 all-reduce.81.cloned.1.call-done
  1731.6 95.5 all-reduce.83.cloned.1.call-done
  1914.5 92.1 all-reduce.85.cloned.1.call-done
  2147.5 95.4 all-reduce.87.cloned.1.call-done
  2330.3 92.1 all-reduce.89.cloned.1.call-done
  2563.2 95.5 all-reduce.91.cloned.1.call-done
  2746.1 92.1 all-reduce.93.cloned.1.call-done
  2979.2 95.6 all-reduce.95.cloned.1.call-done
  3162.1 92.1 all-reduce.97.cloned.1.call-done
  3395.2 95.5 all-reduce.99.cloned.1.call-done
  3578.0 92.1 all-reduce.101.cloned.1.call-done
  3811.0 95.7 all-reduce.103.cloned.1.call-done
  3994.0 92.1 all-reduce.105.cloned.1.call-done
  4227.0 95.7 all-reduce.107.cloned.1.call-done
  4410.0 92.1 all-reduce.109.cloned.1.call-done
  4643.0 95.5 all-reduce.111.cloned.1.call-done
  4825.9 92.2 all-reduce.113.cloned.1.call-done
  5059.0 95.7 all-reduce.115.cloned.1.call-done
  5242.0 92.1 all-reduce.117.cloned.1.call-done
  5475.1 95.5 all-reduce.119.cloned.1.call-done
  5658.0 92.2 all-reduce.121.cloned.1.call-done
  5891.1 95.6 all-reduce.123.cloned.1.call-done
  6074.0 92.1 all-reduce.125.cloned.1.call-done
  6306.9 95.5 all-reduce.127.cloned.1.call-done
  6489.7 92.1 all-reduce.129.cloned.1.call-done
  6722.8 95.6 all-reduce.131.cloned.1.call-done
  6905.7 92.2 all-reduce.133.cloned.1.call-done
  7138.7 95.5 all-reduce.135.cloned.1.call-done
  7321.6 92.1 all-reduce.137.cloned.1.call-done
  7554.6 95.5 all-reduce.139.cloned.1.call-done
  7737.4 92.1 all-reduce.141.cloned.1.call-done
  7970.4 95.6 all-reduce.143.cloned.1.call-done
  8153.3 92.1 all-reduce.145.cloned.1.call-done
  8386.3 95.6 all-reduce.147.cloned.1.call-done
  8569.3 92.1 all-reduce.149.cloned.1.call-done
  8802.3 95.6 all-reduce.151.cloned.1.call-done
  8985.2 92.2 all-reduce.153.cloned.1.call-done
  9218.2 95.7 all-reduce.155.cloned.1.call-done
  9401.2 92.1 all-reduce.157.cloned.1.call-done
  9634.1 95.7 all-reduce.159.cloned.1.call-done
  9817.1 92.1 all-reduce.161.cloned.1.call-done
  10050.1 95.4 all-reduce.163.cloned.1.call-done
  10232.8 92.1 all-reduce.165.cloned.1.call-done
  10465.7 95.8 all-reduce.167.cloned.1.call-done
  10881.8 95.6 all-reduce.171.cloned.1.call-done
  11064.7 92.1 all-reduce.173.cloned.1.call-done
  11297.7 95.6 all-reduce.175.cloned.1.call-done
  11480.7 92.1 all-reduce.177.cloned.1.call-done
  11713.7 95.5 all-reduce.179.cloned.1.call-done
  11896.6 92.1 all-reduce.181.cloned.1.call-done
  12129.5 95.7 all-reduce.183.cloned.1.call-done
  12312.5 92.1 all-reduce.185.cloned.1.call-done
  12545.6 95.5 all-reduce.187.cloned.1.call-done
  12728.4 92.1 all-reduce.189.cloned.1.call-done
  12961.4 95.6 all-reduce.191.cloned.1.call-done
  13144.1 92.1 all-reduce.193.cloned.1.call-done
  13380.8 95.8 all-reduce.195.cloned.1.call-done
  (2742 shorter events, 7858.7 us)
Async XLA Ops:
  68.6 273.9 %all-reduce.69.cloned.1.call-start = ((), (), s32[]{:S(2)}) async-start(), calls=%async_computation.35 | async-start | bytes 524288 | tf_op jit(solution)/shard_map/psum | solution.py:16
  250.3 231.0 %reduce-scatter.38.cloned.1.call-start = ((), (), s32[]{:S(2)}) async-start(), calls=%async_computation.36 | async-start | bytes 2064384 | tf_op jit(solution)/shard_map/reduce_scatter | solution.py:31
  484.0 274.9 %all-reduce.73.cloned.1.call-start = ((), (), s32[]{:S(2)}) async-start(), calls=%async_computation.38 | async-start | bytes 524288 | tf_op jit(solution)/shard_map/psum | solution.py:16
  666.8 230.3 %reduce-scatter.40.cloned.1.call-start = ((), (), s32[]{:S(2)}) async-start(), calls=%async_computation.39 | async-start | bytes 2064384 | tf_op jit(solution)/shard_map/reduce_scatter | solution.py:31
  899.7 275.1 %all-reduce.77.cloned.1.call-start = ((), (), s32[]{:S(2)}) async-start(), calls=%async_computation.41 | async-start | bytes 524288 | tf_op jit(solution)/shard_map/psum | solution.py:16
  1082.6 230.4 %reduce-scatter.42.cloned.1.call-start = ((), (), s32[]{:S(2)}) async-start(), calls=%async_computation.42 | async-start | bytes 2064384 | tf_op jit(solution)/shard_map/reduce_scatter | solution.py:31
  1315.5 275.3 %all-reduce.81.cloned.1.call-start = ((), (), s32[]{:S(2)}) async-start(), calls=%async_computation.44 | async-start | bytes 524288 | tf_op jit(solution)/shard_map/psum | solution.py:16
  1498.6 230.3 %reduce-scatter.44.cloned.1.call-start = ((), (), s32[]{:S(2)}) async-start(), calls=%async_computation.45 | async-start | bytes 2064384 | tf_op jit(solution)/shard_map/reduce_scatter | solution.py:31
  1731.6 275.1 %all-reduce.85.cloned.1.call-start = ((), (), s32[]{:S(2)}) async-start(), calls=%async_computation.47 | async-start | bytes 524288 | tf_op jit(solution)/shard_map/psum | solution.py:16
  1914.5 230.3 %reduce-scatter.46.cloned.1.call-start = ((), (), s32[]{:S(2)}) async-start(), calls=%async_computation.48 | async-start | bytes 2064384 | tf_op jit(solution)/shard_map/reduce_scatter | solution.py:31
  2147.4 275.0 %all-reduce.89.cloned.1.call-start = ((), (), s32[]{:S(2)}) async-start(), calls=%async_computation.50 | async-start | bytes 524288 | tf_op jit(solution)/shard_map/psum | solution.py:16
  2330.2 230.4 %reduce-scatter.48.cloned.1.call-start = ((), (), s32[]{:S(2)}) async-start(), calls=%async_computation.51 | async-start | bytes 2064384 | tf_op jit(solution)/shard_map/reduce_scatter | solution.py:31
  2563.2 275.1 %all-reduce.93.cloned.1.call-start = ((), (), s32[]{:S(2)}) async-start(), calls=%async_computation.53 | async-start | bytes 524288 | tf_op jit(solution)/shard_map/psum | solution.py:16
  2746.0 230.4 %reduce-scatter.50.cloned.1.call-start = ((), (), s32[]{:S(2)}) async-start(), calls=%async_computation.54 | async-start | bytes 2064384 | tf_op jit(solution)/shard_map/reduce_scatter | solution.py:31
  2979.1 275.1 %all-reduce.97.cloned.1.call-start = ((), (), s32[]{:S(2)}) async-start(), calls=%async_computation.56 | async-start | bytes 524288 | tf_op jit(solution)/shard_map/psum | solution.py:16
  3162.1 230.3 %reduce-scatter.52.cloned.1.call-start = ((), (), s32[]{:S(2)}) async-start(), calls=%async_computation.57 | async-start | bytes 2064384 | tf_op jit(solution)/shard_map/reduce_scatter | solution.py:31
  3395.1 275.0 %all-reduce.101.cloned.1.call-start = ((), (), s32[]{:S(2)}) async-start(), calls=%async_computation.59 | async-start | bytes 524288 | tf_op jit(solution)/shard_map/psum | solution.py:16
  3577.9 230.3 %reduce-scatter.54.cloned.1.call-start = ((), (), s32[]{:S(2)}) async-start(), calls=%async_computation.60 | async-start | bytes 2064384 | tf_op jit(solution)/shard_map/reduce_scatter | solution.py:31
  3810.9 275.2 %all-reduce.105.cloned.1.call-start = ((), (), s32[]{:S(2)}) async-start(), calls=%async_computation.62 | async-start | bytes 524288 | tf_op jit(solution)/shard_map/psum | solution.py:16
  3993.9 230.3 %reduce-scatter.56.cloned.1.call-start = ((), (), s32[]{:S(2)}) async-start(), calls=%async_computation.63 | async-start | bytes 2064384 | tf_op jit(solution)/shard_map/reduce_scatter | solution.py:31
  4226.9 275.2 %all-reduce.109.cloned.1.call-start = ((), (), s32[]{:S(2)}) async-start(), calls=%async_computation.65 | async-start | bytes 524288 | tf_op jit(solution)/shard_map/psum | solution.py:16
  4409.9 230.3 %reduce-scatter.58.cloned.1.call-start = ((), (), s32[]{:S(2)}) async-start(), calls=%async_computation.66 | async-start | bytes 2064384 | tf_op jit(solution)/shard_map/reduce_scatter | solution.py:31
  4642.9 275.2 %all-reduce.113.cloned.1.call-start = ((), (), s32[]{:S(2)}) async-start(), calls=%async_computation.68 | async-start | bytes 524288 | tf_op jit(solution)/shard_map/psum | solution.py:16
  4825.8 230.4 %reduce-scatter.60.cloned.1.call-start = ((), (), s32[]{:S(2)}) async-start(), calls=%async_computation.69 | async-start | bytes 2064384 | tf_op jit(solution)/shard_map/reduce_scatter | solution.py:31
  5058.9 275.2 %all-reduce.117.cloned.1.call-start = ((), (), s32[]{:S(2)}) async-start(), calls=%async_computation.71 | async-start | bytes 524288 | tf_op jit(solution)/shard_map/psum | solution.py:16
  5241.9 230.4 %reduce-scatter.62.cloned.1.call-start = ((), (), s32[]{:S(2)}) async-start(), calls=%async_computation.72 | async-start | bytes 2064384 | tf_op jit(solution)/shard_map/reduce_scatter | solution.py:31
  5475.0 275.2 %all-reduce.121.cloned.1.call-start = ((), (), s32[]{:S(2)}) async-start(), calls=%async_computation.74 | async-start | bytes 524288 | tf_op jit(solution)/shard_map/psum | solution.py:16
  5657.9 230.4 %reduce-scatter.64.cloned.1.call-start = ((), (), s32[]{:S(2)}) async-start(), calls=%async_computation.75 | async-start | bytes 2064384 | tf_op jit(solution)/shard_map/reduce_scatter | solution.py:31
  5891.0 275.1 %all-reduce.125.cloned.1.call-start = ((), (), s32[]{:S(2)}) async-start(), calls=%async_computation.77 | async-start | bytes 524288 | tf_op jit(solution)/shard_map/psum | solution.py:16
  6073.9 230.3 %reduce-scatter.66.cloned.1.call-start = ((), (), s32[]{:S(2)}) async-start(), calls=%async_computation.78 | async-start | bytes 2064384 | tf_op jit(solution)/shard_map/reduce_scatter | solution.py:31
  6306.8 275.1 %all-reduce.129.cloned.1.call-start = ((), (), s32[]{:S(2)}) async-start(), calls=%async_computation.80 | async-start | bytes 524288 | tf_op jit(solution)/shard_map/psum | solution.py:16
  6489.7 230.4 %reduce-scatter.68.cloned.1.call-start = ((), (), s32[]{:S(2)}) async-start(), calls=%async_computation.81 | async-start | bytes 2064384 | tf_op jit(solution)/shard_map/reduce_scatter | solution.py:31
  6722.7 275.2 %all-reduce.133.cloned.1.call-start = ((), (), s32[]{:S(2)}) async-start(), calls=%async_computation.83 | async-start | bytes 524288 | tf_op jit(solution)/shard_map/psum | solution.py:16
  6905.6 230.4 %reduce-scatter.70.cloned.1.call-start = ((), (), s32[]{:S(2)}) async-start(), calls=%async_computation.84 | async-start | bytes 2064384 | tf_op jit(solution)/shard_map/reduce_scatter | solution.py:31
  7138.7 275.0 %all-reduce.137.cloned.1.call-start = ((), (), s32[]{:S(2)}) async-start(), calls=%async_computation.86 | async-start | bytes 524288 | tf_op jit(solution)/shard_map/psum | solution.py:16
  7321.5 230.3 %reduce-scatter.72.cloned.1.call-start = ((), (), s32[]{:S(2)}) async-start(), calls=%async_computation.87 | async-start | bytes 2064384 | tf_op jit(solution)/shard_map/reduce_scatter | solution.py:31
  7554.5 275.0 %all-reduce.141.cloned.1.call-start = ((), (), s32[]{:S(2)}) async-start(), calls=%async_computation.89 | async-start | bytes 524288 | tf_op jit(solution)/shard_map/psum | solution.py:16
  7737.3 230.4 %reduce-scatter.74.cloned.1.call-start = ((), (), s32[]{:S(2)}) async-start(), calls=%async_computation.90 | async-start | bytes 2064384 | tf_op jit(solution)/shard_map/reduce_scatter | solution.py:31
  7970.3 275.1 %all-reduce.145.cloned.1.call-start = ((), (), s32[]{:S(2)}) async-start(), calls=%async_computation.92 | async-start | bytes 524288 | tf_op jit(solution)/shard_map/psum | solution.py:16
  8153.2 230.3 %reduce-scatter.76.cloned.1.call-start = ((), (), s32[]{:S(2)}) async-start(), calls=%async_computation.93 | async-start | bytes 2064384 | tf_op jit(solution)/shard_map/reduce_scatter | solution.py:31
  8386.3 275.1 %all-reduce.149.cloned.1.call-start = ((), (), s32[]{:S(2)}) async-start(), calls=%async_computation.95 | async-start | bytes 524288 | tf_op jit(solution)/shard_map/psum | solution.py:16
  8569.2 230.3 %reduce-scatter.78.cloned.1.call-start = ((), (), s32[]{:S(2)}) async-start(), calls=%async_computation.96 | async-start | bytes 2064384 | tf_op jit(solution)/shard_map/reduce_scatter | solution.py:31
  8802.2 275.2 %all-reduce.153.cloned.1.call-start = ((), (), s32[]{:S(2)}) async-start(), calls=%async_computation.98 | async-start | bytes 524288 | tf_op jit(solution)/shard_map/psum | solution.py:16
  8985.1 230.4 %reduce-scatter.80.cloned.1.call-start = ((), (), s32[]{:S(2)}) async-start(), calls=%async_computation.99 | async-start | bytes 2064384 | tf_op jit(solution)/shard_map/reduce_scatter | solution.py:31
  9218.1 275.2 %all-reduce.157.cloned.1.call-start = ((), (), s32[]{:S(2)}) async-start(), calls=%async_computation.101 | async-start | bytes 524288 | tf_op jit(solution)/shard_map/psum | solution.py:16
  9401.2 230.3 %reduce-scatter.82.cloned.1.call-start = ((), (), s32[]{:S(2)}) async-start(), calls=%async_computation.102 | async-start | bytes 2064384 | tf_op jit(solution)/shard_map/reduce_scatter | solution.py:31
  9634.0 275.2 %all-reduce.161.cloned.1.call-start = ((), (), s32[]{:S(2)}) async-start(), calls=%async_computation.104 | async-start | bytes 524288 | tf_op jit(solution)/shard_map/psum | solution.py:16
  9817.0 230.3 %reduce-scatter.84.cloned.1.call-start = ((), (), s32[]{:S(2)}) async-start(), calls=%async_computation.105 | async-start | bytes 2064384 | tf_op jit(solution)/shard_map/reduce_scatter | solution.py:31
  10050.0 274.9 %all-reduce.165.cloned.1.call-start = ((), (), s32[]{:S(2)}) async-start(), calls=%async_computation.107 | async-start | bytes 524288 | tf_op jit(solution)/shard_map/psum | solution.py:16
  10232.7 230.3 %reduce-scatter.86.cloned.1.call-start = ((), (), s32[]{:S(2)}) async-start(), calls=%async_computation.108 | async-start | bytes 2064384 | tf_op jit(solution)/shard_map/reduce_scatter | solution.py:31
  10465.6 275.2 %all-reduce.169.cloned.1.call-start = ((), (), s32[]{:S(2)}) async-start(), calls=%async_computation.110 | async-start | bytes 524288 | tf_op jit(solution)/shard_map/psum | solution.py:16
  10648.7 230.3 %reduce-scatter.88.cloned.1.call-start = ((), (), s32[]{:S(2)}) async-start(), calls=%async_computation.111 | async-start | bytes 2064384 | tf_op jit(solution)/shard_map/reduce_scatter | solution.py:31
  10881.7 275.1 %all-reduce.173.cloned.1.call-start = ((), (), s32[]{:S(2)}) async-start(), calls=%async_computation.113 | async-start | bytes 524288 | tf_op jit(solution)/shard_map/psum | solution.py:16
  11064.6 230.3 %reduce-scatter.90.cloned.1.call-start = ((), (), s32[]{:S(2)}) async-start(), calls=%async_computation.114 | async-start | bytes 2064384 | tf_op jit(solution)/shard_map/reduce_scatter | solution.py:31
  11297.7 275.1 %all-reduce.177.cloned.1.call-start = ((), (), s32[]{:S(2)}) async-start(), calls=%async_computation.116 | async-start | bytes 524288 | tf_op jit(solution)/shard_map/psum | solution.py:16
  11480.6 230.3 %reduce-scatter.92.cloned.1.call-start = ((), (), s32[]{:S(2)}) async-start(), calls=%async_computation.117 | async-start | bytes 2064384 | tf_op jit(solution)/shard_map/reduce_scatter | solution.py:31
  11713.6 275.0 %all-reduce.181.cloned.1.call-start = ((), (), s32[]{:S(2)}) async-start(), calls=%async_computation.119 | async-start | bytes 524288 | tf_op jit(solution)/shard_map/psum | solution.py:16
  11896.5 230.3 %reduce-scatter.94.cloned.1.call-start = ((), (), s32[]{:S(2)}) async-start(), calls=%async_computation.120 | async-start | bytes 2064384 | tf_op jit(solution)/shard_map/reduce_scatter | solution.py:31
  12129.5 275.2 %all-reduce.185.cloned.1.call-start = ((), (), s32[]{:S(2)}) async-start(), calls=%async_computation.122 | async-start | bytes 524288 | tf_op jit(solution)/shard_map/psum | solution.py:16
  12312.5 230.3 %reduce-scatter.96.cloned.1.call-start = ((), (), s32[]{:S(2)}) async-start(), calls=%async_computation.123 | async-start | bytes 2064384 | tf_op jit(solution)/shard_map/reduce_scatter | solution.py:31
  12545.5 275.0 %all-reduce.189.cloned.1.call-start = ((), (), s32[]{:S(2)}) async-start(), calls=%async_computation.125 | async-start | bytes 524288 | tf_op jit(solution)/shard_map/psum | solution.py:16
  12728.3 230.3 %reduce-scatter.98.cloned.1.call-start = ((), (), s32[]{:S(2)}) async-start(), calls=%async_computation.126 | async-start | bytes 2064384 | tf_op jit(solution)/shard_map/reduce_scatter | solution.py:31
  12961.3 274.9 %all-reduce.193.cloned.1.call-start = ((), (), s32[]{:S(2)}) async-start(), calls=%async_computation.128 | async-start | bytes 524288 | tf_op jit(solution)/shard_map/psum | solution.py:16
  13144.1 234.4 %reduce-scatter.100.cloned.1.call-start = ((), (), s32[]{:S(2)}) async-start(), calls=%async_computation.130 | async-start | bytes 2064384
  (325 other events, 16259.6 us)
Sparse Core Ops, SparseCore 0:
  69.8 94.4 all-reduce.66
  250.4 92.0 all-reduce.68
  485.0 94.4 all-reduce.70
  666.9 91.9 all-reduce.72
  900.9 94.3 all-reduce.74
  1082.7 92.0 all-reduce.76
  1316.8 94.4 all-reduce.78
  1498.7 92.0 all-reduce.80
  1732.7 94.4 all-reduce.82
  1914.6 92.0 all-reduce.84
  2148.5 94.4 all-reduce.86
  2330.3 92.0 all-reduce.88
  2564.3 94.4 all-reduce.90
  2746.2 92.0 all-reduce.92
  2980.3 94.4 all-reduce.94
  3162.2 92.0 all-reduce.96
  3396.1 94.4 all-reduce.98
  3578.0 92.0 all-reduce.100
  3812.1 94.4 all-reduce.102
  3994.0 92.0 all-reduce.104
  4228.1 94.4 all-reduce.106
  4410.0 92.0 all-reduce.108
  4644.1 94.4 all-reduce.110
  4825.9 92.1 all-reduce.112
  5060.1 94.4 all-reduce.114
  5242.1 92.0 all-reduce.116
  5476.2 94.4 all-reduce.118
  5658.0 92.1 all-reduce.120
  5892.2 94.4 all-reduce.122
  6074.0 91.9 all-reduce.124
  6307.9 94.4 all-reduce.126
  6489.8 92.0 all-reduce.128
  6723.9 94.4 all-reduce.130
  6905.8 92.1 all-reduce.132
  7139.8 94.4 all-reduce.134
  7321.6 91.9 all-reduce.136
  7555.7 94.3 all-reduce.138
  7737.5 92.0 all-reduce.140
  7971.4 94.4 all-reduce.142
  8153.3 92.0 all-reduce.144
  8387.4 94.4 all-reduce.146
  8569.3 92.0 all-reduce.148
  8803.4 94.4 all-reduce.150
  8985.3 92.1 all-reduce.152
  9219.4 94.4 all-reduce.154
  9401.3 91.9 all-reduce.156
  9635.3 94.4 all-reduce.158
  9817.2 91.9 all-reduce.160
  10051.1 94.3 all-reduce.162
  10232.9 92.0 all-reduce.164
  10466.9 94.4 all-reduce.166
  10882.9 94.4 all-reduce.170
  11064.8 92.0 all-reduce.172
  11298.8 94.4 all-reduce.174
  11480.8 92.0 all-reduce.176
  11714.7 94.4 all-reduce.178
  11896.6 92.0 all-reduce.180
  12130.7 94.4 all-reduce.182
  12312.6 92.0 all-reduce.184
  12546.5 94.4 all-reduce.186
  12728.4 92.0 all-reduce.188
  12962.5 94.4 all-reduce.190
  13144.2 91.9 all-reduce.192
  13382.2 94.4 all-reduce.194
  (34 shorter events, 1048.4 us)
where the time goes:
time: 13500 us
  waiting for transfers between devices  7260 us (54%)
  other arithmetic  4150 us (31%)
  local copies, waits for them, and re-layouts  804 us (6%)
  matrix products  583 us (4%)
  blocking collectives  458 us (3%)
    psum x32, waiting for transfers between devices, orthonormalize(): lax.psum(lax.dot_general(y_low, y_low, ROW_CONTRACT, preferred_element_ty...  3060 us
    psum x32, waiting for transfers between devices, orthonormalize(): lax.psum(lax.dot_general(y_mid, y_mid, ROW_CONTRACT, precision=FULL_PRECI...  2950 us
    another operation x224, other arithmetic, orthonormalize(): chol_two = jnp.linalg.cholesky(gram_two)  1230 us
    another operation x223, other arithmetic, orthonormalize(): chol_one = jnp.linalg.cholesky(gram_one)  1230 us
    reduce_scatter x32, waiting for transfers between devices, apply_operator(): lax.psum_scatter(partial_rows, 'col', scatter_dimension=0, tiled=True)  931 us
    another operation x65, other arithmetic, orthonormalize(): lax.linalg.triangular_solve(chol_one, y_loc, left_side=False, lower=True,...  729 us
    another operation x64, other arithmetic, orthonormalize(): lax.linalg.triangular_solve(chol_two, y_mid, left_side=False, lower=True,...  729 us
    all_gather x33, blocking collectives, apply_operator(): x_column = lax.all_gather(x_moved, 'row', axis=0, tiled=True)  458 us
  transfers between devices with their start and end apart: 131, of which 131 were waited for; matrix products, arithmetic and copies ran while one was open for 0% of the time, Pallas kernels for 0%

commit v1 on v0

v1 whole, which is shorter than its diff:
```python
import functools

import jax
import jax.numpy as jnp
from jax import lax
from jax.experimental import pallas as pl
from jax.experimental.pallas import tpu as pltpu
from jax.sharding import PartitionSpec as P

HI = lax.Precision.HIGHEST
ROW_CONTRACT = (((0,), (0,)), ((), ()))
GRID_AXES = ("row", "col")
NB = 32
FIRST_ERR = 1e-2
SECOND_ERR = 1.6e-7
LINE = (0, 1, -1, 2)
MESH_ID = pl.DeviceIdType.MESH


def factor_panel(panel, start, nb):
    width = panel.shape[1]
    tiles = width // 128
    groups = nb // 8
    p = [[panel[8*v:8*v+8, 128*t:128*t+128] for t in range(tiles)] for v in range(groups)]
    sub = lax.broadcasted_iota(jnp.int32, (8, 128), 0)
    lane = lax.broadcasted_iota(jnp.int32, (8, 128), 1)
    dinv = [None]*groups
    for g in range(groups):
        cols = [start + 8*g + j for j in range(8)]
        b = [[jnp.broadcast_to(p[v][c//128][:, c%128:c%128+1], (8, 128)) for v in range(g, groups)] for c in cols]
        dg = jnp.ones((8, 128), jnp.float32)
        for j in range(8):
            c = cols[j]
            tc = c // 128
            d = jnp.broadcast_to(b[j][0][j:j+1, :], (8, 128))
            inv = 1.0 / d
            dg = jnp.where(sub == j, inv, dg)
            m = [b[j][v]*inv for v in range(groups-g)]
            for q in range(j+1, 8):
                f = jnp.broadcast_to(b[q][0][j:j+1, :], (8, 128))
                b[q] = [b[q][v] - m[v]*f for v in range(groups-g)]
            m[0] = jnp.where(sub > j, m[0], 0.0)
            for t in range(tiles):
                r = jnp.broadcast_to(p[g][t][j:j+1, :], (8, 128))
                if t == tc:
                    r = jnp.where(lane == c % 128, 1.0, r)
                for v in range(g, groups):
                    old = p[v][t]
                    if t == tc:
                        old = jnp.where(lane == c % 128, jnp.where(sub == j, 1.0, 0.0) if v == g else 0.0, old)
                    p[v][t] = old - m[v-g]*r
            for v in range(g):
                p[v][tc] = jnp.where(lane == c % 128, 0.0, p[v][tc])
        dinv[g] = dg
    rows = []
    for v in range(groups):
        s = jnp.sqrt(dinv[v])
        rows.append(jnp.concatenate([p[v][t]*s for t in range(tiles)], axis=1))
    return jnp.concatenate(rows, axis=0)


def chol_inverse(w_ref, nb=NB):
    size = w_ref.shape[0]
    for k in range(size // nb):
        lo, hi = k*nb, (k+1)*nb
        panel = factor_panel(w_ref[lo:hi, :], lo, nb)
        w_ref[lo:hi, :] = panel
        if hi < size:
            upd = lax.dot_general(panel, panel, (((0,), (0,)), ((), ())), precision=HI, preferred_element_type=jnp.float32)
            upd = upd[hi:, :]
            lane = lax.broadcasted_iota(jnp.int32, (size-hi, size), 1)
            old = w_ref[hi:, :]
            old = jnp.where((lane >= lo) & (lane < hi), 0.0, old)
            w_ref[hi:, :] = old - upd


def lower_mask(x):
    r = lax.broadcasted_iota(jnp.int32, x.shape, 0)
    c = lax.broadcasted_iota(jnp.int32, x.shape, 1)
    return jnp.where(r >= c, x, 0.0)


def cholesky_inverse_kernel(g_ref, o_ref, work):
    work[...] = g_ref[...]
    chol_inverse(work)
    o_ref[...] = lower_mask(work[...])


def cholesky_inverse(gram):
    return pl.pallas_call(
        cholesky_inverse_kernel,
        out_shape=jax.ShapeDtypeStruct(gram.shape, jnp.float32),
        in_specs=[pl.BlockSpec(memory_space=pltpu.VMEM)],
        out_specs=pl.BlockSpec(memory_space=pltpu.VMEM),
        scratch_shapes=[pltpu.VMEM(gram.shape, jnp.float32)],
    )(gram)


def apply_inverse(y_loc, factor_inv):
    return lax.dot_general(y_loc, factor_inv, (((1,), (1,)), ((), ())), precision=HI, preferred_element_type=jnp.float32)


def orthonormalize(y_loc, total_rows):
    y_low = y_loc.astype(jnp.bfloat16)
    gram_one = lax.psum(lax.dot_general(y_low, y_low, ROW_CONTRACT, preferred_element_type=jnp.float32), GRID_AXES) / total_rows
    y_mid = apply_inverse(y_loc, cholesky_inverse(gram_one))
    gram_two = lax.psum(lax.dot_general(y_mid, y_mid, ROW_CONTRACT, precision=HI, preferred_element_type=jnp.float32), GRID_AXES) / total_rows
    return apply_inverse(y_mid, cholesky_inverse(gram_two))

def lower_half(err):
    r = lax.broadcasted_iota(jnp.int32, err.shape, 0)
    c = lax.broadcasted_iota(jnp.int32, err.shape, 1)
    return jnp.where(r > c, err, jnp.where(r == c, 0.5 * err, 0.0))


def eye(size):
    return jnp.where(lax.broadcasted_iota(jnp.int32, (size, size), 0) == lax.broadcasted_iota(jnp.int32, (size, size), 1), 1.0, 0.0)


def mul(a, b):
    return jnp.dot(a, b, precision=HI, preferred_element_type=jnp.float32)


def mul_t(a, b):
    return lax.dot_general(a, b, (((1,), (1,)), ((), ())), precision=HI, preferred_element_type=jnp.float32)


def factor_kernel(total_rows, y_ref, g_ref, flag_ref, x_ref, xlow_ref, flag_out, work):
    scale = 1.0 / total_rows
    work[...] = g_ref[0] * scale
    chol_inverse(work)
    first = lower_mask(work[...])
    unit = eye(work.shape[0])
    gram_two = mul_t(mul(first, g_ref[1] * scale), first)
    err = gram_two - unit
    far_one = jnp.where(jnp.sum(err * err) <= FIRST_ERR, 0.0, 1.0)
    second = unit - lower_half(err)
    err = mul_t(mul(second, gram_two), second) - unit
    far_two = jnp.where(jnp.sum(err * err) <= SECOND_ERR, 0.0, 1.0)
    flag_out[...] = jnp.maximum(flag_ref[...], jnp.maximum(far_one, far_two))
    second = second - mul(lower_half(err), second)
    x_val = mul_t(y_ref[...], mul(second, first))
    x_ref[...] = x_val
    xlow_ref[...] = x_val.astype(jnp.bfloat16)


def factor_and_apply(total_rows, y_loc, grams, flag):
    vmem = pl.BlockSpec(memory_space=pltpu.VMEM)
    return pl.pallas_call(
        functools.partial(factor_kernel, total_rows),
        out_shape=(
            jax.ShapeDtypeStruct(y_loc.shape, jnp.float32),
            jax.ShapeDtypeStruct(y_loc.shape, jnp.bfloat16),
            jax.ShapeDtypeStruct(flag.shape, jnp.float32),
        ),
        in_specs=[vmem] * 3,
        out_specs=(vmem,) * 3,
        scratch_shapes=[pltpu.VMEM(grams.shape[1:], jnp.float32)],
        name="factor_and_apply",
    )(y_loc, grams, flag)


def sweep_kernel(dims, final, shift_ref, index_ref, a_hbm, xlow_ref, x_ref, y_ref, g_ref,
                 a_buf, xbuf, acc, gloc, rhalf, ghalf, slots, red, gsum,
                 a_sem, send_near, recv_near, send_far, recv_far, send_line, recv_line, send_end, recv_end,
                 send_core, recv_core, send_half, recv_half, send_rs, recv_rs, send_bc, recv_bc, send_out, recv_out):
    rows_y, cols, rows = dims
    chips_x = cols // 2
    half = rows // 2
    row, col = lax.axis_index("row"), lax.axis_index("col")
    chip, core = lax.div(col, 2), lax.rem(col, 2)
    size = x_ref.shape[1]
    lanes = size // 2
    part = size // 2
    strip = part // (rows_y * chips_x)

    def place(dx, dy):
        return lax.rem(chip + dx + chips_x, chips_x), lax.rem(row + dy + rows_y, rows_y)

    def device(dx, dy, flip=False):
        px, py = place(dx, dy)
        return {"row": py, "col": px * 2 + ((1 - core) if flip else core)}

    def slot(dx, dy):
        px, py = place(dx, dy)
        return py * chips_x + px

    def axis_pair(h, u, v):
        return (u, v) if h == 0 else (v, u)

    plane = [(dx, dy) for dy in LINE for dx in LINE if (dx, dy) != (0, 0)]
    barrier = pltpu.get_barrier_semaphore()
    for dx, dy in plane:
        pl.semaphore_signal(barrier, inc=1, device_id=device(dx, dy), device_id_type=MESH_ID)
    pl.semaphore_signal(barrier, inc=1, device_id=device(0, 0, True), device_id_type=MESH_ID)
    pl.semaphore_wait(barrier, len(plane) + 1)

    load_a = pltpu.make_async_copy(a_hbm, a_buf, a_sem)
    load_a.start()

    sent = []

    def send(src, dst, ssem, rsem, dev):
        copy = pltpu.make_async_remote_copy(src_ref=src, dst_ref=dst, send_sem=ssem, recv_sem=rsem, device_id=dev, device_id_type=MESH_ID)
        copy.start()
        sent.append(copy)
        return copy

    base = pl.multiple_of(core * rows, 32)

    def unit(h, dx, dy, lane=None):
        where = pl.ds(pl.multiple_of(base + h * half, 16), half)
        if lane is None:
            return xbuf.at[slot(dx, dy), where, :]
        return xbuf.at[slot(dx, dy), where, pl.ds(lane * lanes, lanes)]

    def own(h):
        return xlow_ref.at[pl.ds(h * half, half), :]

    near, far, line, end, cross = {}, {}, {}, {}, {}

    def start_near(h, d):
        near[h, d] = send(own(h), unit(h, 0, 0), send_near.at[h, (d + 1) // 2], recv_near.at[h, (d + 1) // 2], device(*axis_pair(h, d, 0)))

    def start_far(h, d):
        piece = unit(h, *axis_pair(h, -d, 0), lane=(d + 1) // 2)
        far[h, d] = send(piece, piece, send_far.at[h, (d + 1) // 2], recv_far.at[h, (d + 1) // 2], device(*axis_pair(h, d, 0)))

    def start_line(h, u):
        for d in (1, -1):
            piece = unit(h, *axis_pair(h, u, 0))
            line[h, u, d] = send(own(h) if u == 0 else piece, piece, send_line.at[h, u + 1, (d + 1) // 2], recv_line.at[h, u + 1, (d + 1) // 2],
                                 device(*axis_pair(h, 0, d)))

    def start_end(h, u, d):
        piece = unit(h, *axis_pair(h, u, -d), lane=(d + 1) // 2)
        end[h, u, d] = send(piece, piece, send_end.at[h, u + 1, (d + 1) // 2], recv_end.at[h, u + 1, (d + 1) // 2], device(*axis_pair(h, 0, d)))

    def start_cross(dx, dy):
        block = xbuf.at[slot(dx, dy), pl.ds(base, rows), :]
        index = (dy + 1) * 4 + dx + 1
        cross[dx, dy] = send(xlow_ref if (dx, dy) == (0, 0) else block, block, send_core.at[index], recv_core.at[index], device(0, 0, True))

    def product(dx, dy, first=False):
        cross[dx, dy].wait_recv()
        term = jnp.dot(a_buf[slot(dx, dy)], xbuf[slot(dx, dy)], preferred_element_type=jnp.float32)
        acc[...] = term if first else acc[...] + term

    for d in (1, -1):
        for h in (0, 1):
            start_near(h, d)
    for h in (0, 1):
        start_line(h, 0)
    start_cross(0, 0)
    xbuf[slot(0, 0), pl.ds(base, rows), :] = xlow_ref[...]
    for d in (1, -1):
        for h in (0, 1):
            near[h, d].wait_recv()
            start_far(h, d)
            start_line(h, -d)
    for d in (1, -1):
        for h in (0, 1):
            line[h, 0, d].wait_recv()
            start_end(h, 0, d)
    for d in (1, -1):
        start_cross(d, 0)
        start_cross(0, d)
    load_a.wait()
    product(0, 0, first=True)
    for h in (0, 1):
        for d in (1, -1):
            far[h, d].wait_recv()
        start_line(h, 2)
    for u in (1, -1):
        for d in (1, -1):
            for h in (0, 1):
                line[h, u, d].wait_recv()
                start_end(h, u, d)
    for u in (1, -1):
        for d in (1, -1):
            start_cross(u, d)
    for d in (1, -1):
        product(d, 0)
        product(0, d)
    for h in (0, 1):
        for d in (1, -1):
            end[h, 0, d].wait_recv()
    start_cross(2, 0)
    start_cross(0, 2)
    for d in (1, -1):
        for h in (0, 1):
            line[h, 2, d].wait_recv()
            start_end(h, 2, d)
    for u in (1, -1):
        for d in (1, -1):
            product(u, d)
    for u in (1, -1):
        for h in (0, 1):
            for d in (1, -1):
                end[h, u, d].wait_recv()
    for u in (1, -1):
        start_cross(2, u)
        start_cross(u, 2)
    product(2, 0)
    product(0, 2)
    for h in (0, 1):
        for d in (1, -1):
            end[h, 2, d].wait_recv()
    start_cross(2, 2)
    for u in (1, -1):
        product(2, u)
        product(u, 2)
    product(2, 2)

    if final:
        y_ref[...] = acc[...]
        gloc[0] = lax.dot_general(x_ref[...], acc[...], ROW_CONTRACT, precision=HI, preferred_element_type=jnp.float32)
    else:
        y_val = acc[...] - shift_ref[index_ref[0]] * x_ref[...]
        y_ref[...] = y_val
        y_low = y_val.astype(jnp.bfloat16)
        gloc[0] = lax.dot_general(y_low, y_low, ROW_CONTRACT, preferred_element_type=jnp.float32)
        gloc[1] = lax.dot_general(y_val, y_val, ROW_CONTRACT, precision=HI, preferred_element_type=jnp.float32)

    kept = pl.ds(pl.multiple_of(core * part, 8), part)
    given = pl.ds(pl.multiple_of((1 - core) * part, 8), part)
    send(gloc.at[:, given, :], rhalf, send_half, recv_half, device(0, 0, True)).wait_recv()
    ghalf[...] = gloc[:, kept, :] + rhalf[...]
    mine = slot(0, 0)
    waits = []
    for n, (dx, dy) in enumerate(plane):
        rows_of = pl.ds(pl.multiple_of(slot(dx, dy) * strip, 8), strip)
        waits.append(send(ghalf.at[:, rows_of, :], slots.at[mine], send_rs.at[n], recv_rs.at[n], device(dx, dy)))
    slots[mine] = ghalf[:, pl.ds(pl.multiple_of(mine * strip, 8), strip), :]
    for copy in waits:
        copy.wait_recv()
    red[...] = jnp.sum(slots[...], axis=0)
    waits = []
    mine_rows = pl.ds(pl.multiple_of(core * part + mine * strip, 8), strip)
    for n, (dx, dy) in enumerate(plane):
        waits.append(send(red, gsum.at[:, mine_rows, :], send_bc.at[n], recv_bc.at[n], device(dx, dy)))
    gsum[:, mine_rows, :] = red[...]
    for copy in waits:
        copy.wait_recv()
    send(gsum.at[:, kept, :], gsum.at[:, kept, :], send_out, recv_out, device(0, 0, True)).wait_recv()
    g_ref[...] = gsum[...]
    for copy in sent:
        copy.wait_send()


def group_product(dims, final, shifts, index, a_blocks, x_low, x_loc):
    rows_y, cols, rows = dims
    size = x_loc.shape[1]
    chips = rows_y * cols // 2
    grams = 1 if final else 2
    dma = pltpu.SemaphoreType.DMA
    vmem = pl.BlockSpec(memory_space=pltpu.VMEM)
    smem = pl.BlockSpec(memory_space=pltpu.SMEM)
    peers = chips - 1
    return pl.pallas_call(
        functools.partial(sweep_kernel, dims, final),
        out_shape=(jax.ShapeDtypeStruct((rows, size), jnp.float32), jax.ShapeDtypeStruct((grams, size, size), jnp.float32)),
        in_specs=[smem, smem, pl.BlockSpec(memory_space=pl.ANY), vmem, vmem],
        out_specs=(vmem, vmem),
        scratch_shapes=[
            pltpu.VMEM(a_blocks.shape, jnp.bfloat16),
            pltpu.VMEM((chips, 2 * rows, size), jnp.bfloat16),
            pltpu.VMEM((rows, size), jnp.float32),
            pltpu.VMEM((grams, size, size), jnp.float32),
            pltpu.VMEM((grams, size // 2, size), jnp.float32),
            pltpu.VMEM((grams, size // 2, size), jnp.float32),
            pltpu.VMEM((chips, grams, size // 2 // chips, size), jnp.float32),
            pltpu.VMEM((grams, size // 2 // chips, size), jnp.float32),
            pltpu.VMEM((grams, size, size), jnp.float32),
            dma,
            dma((2, 2)), dma((2, 2)), dma((2, 2)), dma((2, 2)),
            dma((2, 4, 2)), dma((2, 4, 2)), dma((2, 4, 2)), dma((2, 4, 2)),
            dma((16,)), dma((16,)), dma, dma,
            dma((peers,)), dma((peers,)), dma((peers,)), dma((peers,)), dma, dma,
        ],
        compiler_params=pltpu.CompilerParams(collective_id=1 if final else 0, has_side_effects=True, vmem_limit_bytes=56 * 2**20),
        name="final_product" if final else "sweep_product",
    )(shifts, index, a_blocks, x_low, x_loc)


def solution(mesh):
    row_count = mesh.shape["row"]
    col_count = mesh.shape["col"]

    def apply_operator(a_rows, x_loc):
        x_full = lax.all_gather(x_loc.astype(jnp.bfloat16), GRID_AXES, axis=0, tiled=True)
        return jnp.dot(a_rows, x_full, preferred_element_type=jnp.float32)

    def careful_program(a_rows, x_loc, shift_vec, total_rows):
        def sweep(sweep_idx, x_cur):
            applied = apply_operator(a_rows, x_cur)
            return orthonormalize(applied - shift_vec[sweep_idx] * x_cur, total_rows)

        x_loc = lax.fori_loop(0, shift_vec.shape[0], sweep, x_loc)
        applied = apply_operator(a_rows, x_loc)
        local_part = lax.dot_general(x_loc, applied, ROW_CONTRACT, precision=HI, preferred_element_type=jnp.float32)
        return x_loc, lax.psum(local_part, GRID_AXES) / total_rows

    def local_program(a_blk, x_start, shift_vec):
        total_rows = a_blk.shape[0] * row_count
        rows = x_start.shape[0]
        dims = (row_count, col_count, rows)
        a_rows = lax.all_to_all(a_blk, "col", split_axis=0, concat_axis=1, tiled=True)
        a_blocks = a_rows.reshape(rows, row_count * col_count // 2, 2 * rows).transpose(1, 0, 2)

        def sweep(sweep_idx, carry):
            x_loc, x_low, flag = carry
            y_loc, grams = group_product(dims, False, shift_vec, jnp.full((1,), sweep_idx, jnp.int32), a_blocks, x_low, x_loc)
            return factor_and_apply(total_rows, y_loc, grams, flag)

        start = (x_start, x_start.astype(jnp.bfloat16), jnp.zeros((8, 128), jnp.float32))
        x_loc, x_low, flag = lax.fori_loop(0, shift_vec.shape[0], sweep, start)
        _, total = group_product(dims, True, shift_vec, jnp.zeros((1,), jnp.int32), a_blocks, x_low, x_loc)
        return lax.cond(
            flag[0, 0] > 0.0,
            lambda: careful_program(a_rows, x_start, shift_vec, total_rows),
            lambda: (x_loc, total[0] / total_rows),
        )

    return jax.shard_map(
        local_program,
        mesh=mesh,
        in_specs=(P(("batch", "row"), "col"), P(("batch", "row", "col"), None), P("batch")),
        out_specs=(P(("batch", "row", "col"), None), P("batch", None)),
        check_vma=False,
    )
```

time: 13500 us -> 1920 us (0.14)
  waiting for transfers between devices: 7260 us -> 36 us
  other arithmetic: 4150 us -> 1.68 us
  Pallas kernels: 0 us -> 1800 us
  local copies, waits for them, and re-layouts: 804 us -> 39.1 us
  matrix products: 583 us -> 0 us
  blocking collectives: 458 us -> 0 us
    psum x65 -> x0, waiting for transfers between devices: 6100 us -> none  [the longest x32 3060 us: orthonormalize(): lax.psum(lax.dot_general(y_low, y_low, ROW_CONTRACT, preferred_element_ty...]
    another operation x576 -> x0, other arithmetic: 3910 us -> none  [the longest x224 1230 us: orthonormalize(): chol_two = jnp.linalg.cholesky(gram_two)]
    pallas_call x0 -> x65, Pallas kernels: none -> 1800 us  [the longest x33 1340 us: group_product(): pl.pallas_call(functools.partial(sweep_kernel, dims, final), out_shape=(j...]
    reduce_scatter x32 -> x0, waiting for transfers between devices: 931 us -> none  [apply_operator(): lax.psum_scatter(partial_rows, 'col', scatter_dimension=0, tiled=True)]
    another operation x577 -> x0, local copies, waits for them, and re-layouts: 620 us -> none  [the longest x257 308 us: orthonormalize(): lax.linalg.triangular_solve(chol_one, y_loc, left_side=False, lower=True,...]
    all_gather x33 -> x0, blocking collectives: 458 us -> none  [apply_operator(): x_column = lax.all_gather(x_moved, 'row', axis=0, tiled=True)]
    another operation x320 -> x0, matrix products: 430 us -> none  [the longest x64 109 us: orthonormalize(): chol_two = jnp.linalg.cholesky(gram_two)]
    ppermute x33 -> x0, waiting for transfers between devices: 196 us -> none  [apply_operator(): x_moved = lax.ppermute(x_low, GRID_AXES, perm_pairs)]
  transfers between devices with their start and end apart: 131 -> 1, of which waited for: 131 -> 1; matrix products, arithmetic and copies ran while one was open for 0% -> 0% of each run, Pallas kernels for 0% -> 0%
where the time goes in v1:
time: 1920 us; the launch traced here: 1900 us
  Pallas kernels  1800 us (94%)
  local copies, waits for them, and re-layouts  39.1 us (2%)
  waiting for transfers between devices  36 us (2%)
    pallas_call x33, Pallas kernels, group_product(): pl.pallas_call(functools.partial(sweep_kernel, dims, final), out_shape=(j...  1340 us
    pallas_call x32, Pallas kernels, factor_and_apply(): pl.pallas_call(functools.partial(factor_kernel, total_rows), out_shape=(j...  469 us
  transfers between devices with their start and end apart: 1, of which 1 were waited for; matrix products, arithmetic and copies ran while one was open for 0% of the time, Pallas kernels for 0%

profile of v1, /device:TPU:97, one launch (start us, length us, event | category | flops | bytes accessed | tf_op | source)
XLA Modules:
  0.0 1903.8 jit_solution(5406362963851856110)
XLA Ops:
  16.7 36.0 %all-to-all-done = bf16[8,224,896]{2,1,0:T(8,128)(2,1)S(1)} async-done(((bf16[8,224,896]{2,1,0:T(8,128)(2,1)}), bf16[8,224,896]{2,1,0:T(8,128)(2,1)S(1)}, u32[]{:S(2)}, u32[]{:S(2)}) %all-to-all-start) | async-done | bytes 3211296 | tf_op jit(solution)/shard_map/all_to_all | solution.py:408
  68.8 1787.1 %while.30 = (s32[]{:T(128)}, f32[224,256]{1,0:T(8,128)S(1)}, bf16[224,256]{1,0:T(8,128)(2,1)S(1)}, f32[8,128]{1,0:T(8,128)}, f32[32]{0:T(128)}, /*index=5*/bf16[16,224,448]{2,1,0:T(8,128)(2,1)}, s32[]{:T(128)}) while((s32[]{:T(128)}, f32[224,256]{1,0:T(8,128)S(1)}, bf16[224,256]{1,0:T(8,128)(2,1)S(1)}, f32[8,128]{1,0:T(8,128)}, f32[32]{0:T(128)}, ...), condition=%wide.region_1.0_spmd, body=%wide.region_0.0_spmd.sunk | while | flops 2 | bytes 24681 | solution.py:417
  69.0 42.1 %sweep_product.5 = (f32[224,256]{1,0:T(8,128)}, f32[2,256,256]{2,1,0:T(8,128)}) custom-call(f32[32]{0:T(128)} %get-tuple-element.340.shift_ref, s32[1]{0:T(128)} %bitcast.34.index_ref, bf16[16,224,448]{2,1,0:T(8,128)(2,1)} %get-tuple-element.341.a_hbm, bf16[224,256]{1,0:T(8,128)(2,1)S(1)} %get-tuple-element.331.xlow_ref, f32[224,256]{1,0:T(8,128)S(1)} %get-tuple-element.330.x_ref), custom_call_target="tpu_custom_call" | custom-call | tf_op jit(solution)/shard_map/while/body/eval_jaxpr/sweep_product/pallas_call | solution.py:360
  111.7 14.6 factor_and_apply.5
  126.3 40.3 %sweep_product.5 = (f32[224,256]{1,0:T(8,128)}, f32[2,256,256]{2,1,0:T(8,128)}) custom-call(f32[32]{0:T(128)} %get-tuple-element.340.shift_ref, s32[1]{0:T(128)} %bitcast.34.index_ref, bf16[16,224,448]{2,1,0:T(8,128)(2,1)} %get-tuple-element.341.a_hbm, bf16[224,256]{1,0:T(8,128)(2,1)S(1)} %get-tuple-element.331.xlow_ref, f32[224,256]{1,0:T(8,128)S(1)} %get-tuple-element.330.x_ref), custom_call_target="tpu_custom_call" | custom-call | tf_op jit(solution)/shard_map/while/body/eval_jaxpr/sweep_product/pallas_call | solution.py:360
  167.3 14.6 factor_and_apply.5
  182.0 40.3 %sweep_product.5 = (f32[224,256]{1,0:T(8,128)}, f32[2,256,256]{2,1,0:T(8,128)}) custom-call(f32[32]{0:T(128)} %get-tuple-element.340.shift_ref, s32[1]{0:T(128)} %bitcast.34.index_ref, bf16[16,224,448]{2,1,0:T(8,128)(2,1)} %get-tuple-element.341.a_hbm, bf16[224,256]{1,0:T(8,128)(2,1)S(1)} %get-tuple-element.331.xlow_ref, f32[224,256]{1,0:T(8,128)S(1)} %get-tuple-element.330.x_ref), custom_call_target="tpu_custom_call" | custom-call | tf_op jit(solution)/shard_map/while/body/eval_jaxpr/sweep_product/pallas_call | solution.py:360
  222.9 14.6 factor_and_apply.5
  237.6 40.5 %sweep_product.5 = (f32[224,256]{1,0:T(8,128)}, f32[2,256,256]{2,1,0:T(8,128)}) custom-call(f32[32]{0:T(128)} %get-tuple-element.340.shift_ref, s32[1]{0:T(128)} %bitcast.34.index_ref, bf16[16,224,448]{2,1,0:T(8,128)(2,1)} %get-tuple-element.341.a_hbm, bf16[224,256]{1,0:T(8,128)(2,1)S(1)} %get-tuple-element.331.xlow_ref, f32[224,256]{1,0:T(8,128)S(1)} %get-tuple-element.330.x_ref), custom_call_target="tpu_custom_call" | custom-call | tf_op jit(solution)/shard_map/while/body/eval_jaxpr/sweep_product/pallas_call | solution.py:360
  293.4 40.5 %sweep_product.5 = (f32[224,256]{1,0:T(8,128)}, f32[2,256,256]{2,1,0:T(8,128)}) custom-call(f32[32]{0:T(128)} %get-tuple-element.340.shift_ref, s32[1]{0:T(128)} %bitcast.34.index_ref, bf16[16,224,448]{2,1,0:T(8,128)(2,1)} %get-tuple-element.341.a_hbm, bf16[224,256]{1,0:T(8,128)(2,1)S(1)} %get-tuple-element.331.xlow_ref, f32[224,256]{1,0:T(8,128)S(1)} %get-tuple-element.330.x_ref), custom_call_target="tpu_custom_call" | custom-call | tf_op jit(solution)/shard_map/while/body/eval_jaxpr/sweep_product/pallas_call | solution.py:360
  334.5 14.6 factor_and_apply.5
  349.2 40.5 %sweep_product.5 = (f32[224,256]{1,0:T(8,128)}, f32[2,256,256]{2,1,0:T(8,128)}) custom-call(f32[32]{0:T(128)} %get-tuple-element.340.shift_ref, s32[1]{0:T(128)} %bitcast.34.index_ref, bf16[16,224,448]{2,1,0:T(8,128)(2,1)} %get-tuple-element.341.a_hbm, bf16[224,256]{1,0:T(8,128)(2,1)S(1)} %get-tuple-element.331.xlow_ref, f32[224,256]{1,0:T(8,128)S(1)} %get-tuple-element.330.x_ref), custom_call_target="tpu_custom_call" | custom-call | tf_op jit(solution)/shard_map/while/body/eval_jaxpr/sweep_product/pallas_call | solution.py:360
  390.3 14.6 factor_and_apply.5
  405.0 40.5 %sweep_product.5 = (f32[224,256]{1,0:T(8,128)}, f32[2,256,256]{2,1,0:T(8,128)}) custom-call(f32[32]{0:T(128)} %get-tuple-element.340.shift_ref, s32[1]{0:T(128)} %bitcast.34.index_ref, bf16[16,224,448]{2,1,0:T(8,128)(2,1)} %get-tuple-element.341.a_hbm, bf16[224,256]{1,0:T(8,128)(2,1)S(1)} %get-tuple-element.331.xlow_ref, f32[224,256]{1,0:T(8,128)S(1)} %get-tuple-element.330.x_ref), custom_call_target="tpu_custom_call" | custom-call | tf_op jit(solution)/shard_map/while/body/eval_jaxpr/sweep_product/pallas_call | solution.py:360
  446.1 14.6 factor_and_apply.5
  460.8 40.5 %sweep_product.5 = (f32[224,256]{1,0:T(8,128)}, f32[2,256,256]{2,1,0:T(8,128)}) custom-call(f32[32]{0:T(128)} %get-tuple-element.340.shift_ref, s32[1]{0:T(128)} %bitcast.34.index_ref, bf16[16,224,448]{2,1,0:T(8,128)(2,1)} %get-tuple-element.341.a_hbm, bf16[224,256]{1,0:T(8,128)(2,1)S(1)} %get-tuple-element.331.xlow_ref, f32[224,256]{1,0:T(8,128)S(1)} %get-tuple-element.330.x_ref), custom_call_target="tpu_custom_call" | custom-call | tf_op jit(solution)/shard_map/while/body/eval_jaxpr/sweep_product/pallas_call | solution.py:360
  501.9 14.6 factor_and_apply.5
  516.6 40.5 %sweep_product.5 = (f32[224,256]{1,0:T(8,128)}, f32[2,256,256]{2,1,0:T(8,128)}) custom-call(f32[32]{0:T(128)} %get-tuple-element.340.shift_ref, s32[1]{0:T(128)} %bitcast.34.index_ref, bf16[16,224,448]{2,1,0:T(8,128)(2,1)} %get-tuple-element.341.a_hbm, bf16[224,256]{1,0:T(8,128)(2,1)S(1)} %get-tuple-element.331.xlow_ref, f32[224,256]{1,0:T(8,128)S(1)} %get-tuple-element.330.x_ref), custom_call_target="tpu_custom_call" | custom-call | tf_op jit(solution)/shard_map/while/body/eval_jaxpr/sweep_product/pallas_call | solution.py:360
  572.4 40.5 %sweep_product.5 = (f32[224,256]{1,0:T(8,128)}, f32[2,256,256]{2,1,0:T(8,128)}) custom-call(f32[32]{0:T(128)} %get-tuple-element.340.shift_ref, s32[1]{0:T(128)} %bitcast.34.index_ref, bf16[16,224,448]{2,1,0:T(8,128)(2,1)} %get-tuple-element.341.a_hbm, bf16[224,256]{1,0:T(8,128)(2,1)S(1)} %get-tuple-element.331.xlow_ref, f32[224,256]{1,0:T(8,128)S(1)} %get-tuple-element.330.x_ref), custom_call_target="tpu_custom_call" | custom-call | tf_op jit(solution)/shard_map/while/body/eval_jaxpr/sweep_product/pallas_call | solution.py:360
  628.2 40.5 %sweep_product.5 = (f32[224,256]{1,0:T(8,128)}, f32[2,256,256]{2,1,0:T(8,128)}) custom-call(f32[32]{0:T(128)} %get-tuple-element.340.shift_ref, s32[1]{0:T(128)} %bitcast.34.index_ref, bf16[16,224,448]{2,1,0:T(8,128)(2,1)} %get-tuple-element.341.a_hbm, bf16[224,256]{1,0:T(8,128)(2,1)S(1)} %get-tuple-element.331.xlow_ref, f32[224,256]{1,0:T(8,128)S(1)} %get-tuple-element.330.x_ref), custom_call_target="tpu_custom_call" | custom-call | tf_op jit(solution)/shard_map/while/body/eval_jaxpr/sweep_product/pallas_call | solution.py:360
  669.4 14.6 factor_and_apply.5
  684.0 40.5 %sweep_product.5 = (f32[224,256]{1,0:T(8,128)}, f32[2,256,256]{2,1,0:T(8,128)}) custom-call(f32[32]{0:T(128)} %get-tuple-element.340.shift_ref, s32[1]{0:T(128)} %bitcast.34.index_ref, bf16[16,224,448]{2,1,0:T(8,128)(2,1)} %get-tuple-element.341.a_hbm, bf16[224,256]{1,0:T(8,128)(2,1)S(1)} %get-tuple-element.331.xlow_ref, f32[224,256]{1,0:T(8,128)S(1)} %get-tuple-element.330.x_ref), custom_call_target="tpu_custom_call" | custom-call | tf_op jit(solution)/shard_map/while/body/eval_jaxpr/sweep_product/pallas_call | solution.py:360
  725.1 14.6 factor_and_apply.5
  739.8 40.5 %sweep_product.5 = (f32[224,256]{1,0:T(8,128)}, f32[2,256,256]{2,1,0:T(8,128)}) custom-call(f32[32]{0:T(128)} %get-tuple-element.340.shift_ref, s32[1]{0:T(128)} %bitcast.34.index_ref, bf16[16,224,448]{2,1,0:T(8,128)(2,1)} %get-tuple-element.341.a_hbm, bf16[224,256]{1,0:T(8,128)(2,1)S(1)} %get-tuple-element.331.xlow_ref, f32[224,256]{1,0:T(8,128)S(1)} %get-tuple-element.330.x_ref), custom_call_target="tpu_custom_call" | custom-call | tf_op jit(solution)/shard_map/while/body/eval_jaxpr/sweep_product/pallas_call | solution.py:360
  780.9 14.6 factor_and_apply.5
  795.6 40.5 %sweep_product.5 = (f32[224,256]{1,0:T(8,128)}, f32[2,256,256]{2,1,0:T(8,128)}) custom-call(f32[32]{0:T(128)} %get-tuple-element.340.shift_ref, s32[1]{0:T(128)} %bitcast.34.index_ref, bf16[16,224,448]{2,1,0:T(8,128)(2,1)} %get-tuple-element.341.a_hbm, bf16[224,256]{1,0:T(8,128)(2,1)S(1)} %get-tuple-element.331.xlow_ref, f32[224,256]{1,0:T(8,128)S(1)} %get-tuple-element.330.x_ref), custom_call_target="tpu_custom_call" | custom-call | tf_op jit(solution)/shard_map/while/body/eval_jaxpr/sweep_product/pallas_call | solution.py:360
  836.7 14.6 factor_and_apply.5
  851.4 40.5 %sweep_product.5 = (f32[224,256]{1,0:T(8,128)}, f32[2,256,256]{2,1,0:T(8,128)}) custom-call(f32[32]{0:T(128)} %get-tuple-element.340.shift_ref, s32[1]{0:T(128)} %bitcast.34.index_ref, bf16[16,224,448]{2,1,0:T(8,128)(2,1)} %get-tuple-element.341.a_hbm, bf16[224,256]{1,0:T(8,128)(2,1)S(1)} %get-tuple-element.331.xlow_ref, f32[224,256]{1,0:T(8,128)S(1)} %get-tuple-element.330.x_ref), custom_call_target="tpu_custom_call" | custom-call | tf_op jit(solution)/shard_map/while/body/eval_jaxpr/sweep_product/pallas_call | solution.py:360
  892.5 14.6 factor_and_apply.5
  907.2 40.5 %sweep_product.5 = (f32[224,256]{1,0:T(8,128)}, f32[2,256,256]{2,1,0:T(8,128)}) custom-call(f32[32]{0:T(128)} %get-tuple-element.340.shift_ref, s32[1]{0:T(128)} %bitcast.34.index_ref, bf16[16,224,448]{2,1,0:T(8,128)(2,1)} %get-tuple-element.341.a_hbm, bf16[224,256]{1,0:T(8,128)(2,1)S(1)} %get-tuple-element.331.xlow_ref, f32[224,256]{1,0:T(8,128)S(1)} %get-tuple-element.330.x_ref), custom_call_target="tpu_custom_call" | custom-call | tf_op jit(solution)/shard_map/while/body/eval_jaxpr/sweep_product/pallas_call | solution.py:360
  948.3 14.6 factor_and_apply.5
  963.0 40.5 %sweep_product.5 = (f32[224,256]{1,0:T(8,128)}, f32[2,256,256]{2,1,0:T(8,128)}) custom-call(f32[32]{0:T(128)} %get-tuple-element.340.shift_ref, s32[1]{0:T(128)} %bitcast.34.index_ref, bf16[16,224,448]{2,1,0:T(8,128)(2,1)} %get-tuple-element.341.a_hbm, bf16[224,256]{1,0:T(8,128)(2,1)S(1)} %get-tuple-element.331.xlow_ref, f32[224,256]{1,0:T(8,128)S(1)} %get-tuple-element.330.x_ref), custom_call_target="tpu_custom_call" | custom-call | tf_op jit(solution)/shard_map/while/body/eval_jaxpr/sweep_product/pallas_call | solution.py:360
  1004.1 14.6 factor_and_apply.5
  1018.8 40.5 %sweep_product.5 = (f32[224,256]{1,0:T(8,128)}, f32[2,256,256]{2,1,0:T(8,128)}) custom-call(f32[32]{0:T(128)} %get-tuple-element.340.shift_ref, s32[1]{0:T(128)} %bitcast.34.index_ref, bf16[16,224,448]{2,1,0:T(8,128)(2,1)} %get-tuple-element.341.a_hbm, bf16[224,256]{1,0:T(8,128)(2,1)S(1)} %get-tuple-element.331.xlow_ref, f32[224,256]{1,0:T(8,128)S(1)} %get-tuple-element.330.x_ref), custom_call_target="tpu_custom_call" | custom-call | tf_op jit(solution)/shard_map/while/body/eval_jaxpr/sweep_product/pallas_call | solution.py:360
  1059.9 14.6 factor_and_apply.5
  1074.6 40.5 %sweep_product.5 = (f32[224,256]{1,0:T(8,128)}, f32[2,256,256]{2,1,0:T(8,128)}) custom-call(f32[32]{0:T(128)} %get-tuple-element.340.shift_ref, s32[1]{0:T(128)} %bitcast.34.index_ref, bf16[16,224,448]{2,1,0:T(8,128)(2,1)} %get-tuple-element.341.a_hbm, bf16[224,256]{1,0:T(8,128)(2,1)S(1)} %get-tuple-element.331.xlow_ref, f32[224,256]{1,0:T(8,128)S(1)} %get-tuple-element.330.x_ref), custom_call_target="tpu_custom_call" | custom-call | tf_op jit(solution)/shard_map/while/body/eval_jaxpr/sweep_product/pallas_call | solution.py:360
  1115.7 14.6 factor_and_apply.5
  1130.4 40.5 %sweep_product.5 = (f32[224,256]{1,0:T(8,128)}, f32[2,256,256]{2,1,0:T(8,128)}) custom-call(f32[32]{0:T(128)} %get-tuple-element.340.shift_ref, s32[1]{0:T(128)} %bitcast.34.index_ref, bf16[16,224,448]{2,1,0:T(8,128)(2,1)} %get-tuple-element.341.a_hbm, bf16[224,256]{1,0:T(8,128)(2,1)S(1)} %get-tuple-element.331.xlow_ref, f32[224,256]{1,0:T(8,128)S(1)} %get-tuple-element.330.x_ref), custom_call_target="tpu_custom_call" | custom-call | tf_op jit(solution)/shard_map/while/body/eval_jaxpr/sweep_product/pallas_call | solution.py:360
  1171.6 14.6 factor_and_apply.5
  1186.2 40.5 %sweep_product.5 = (f32[224,256]{1,0:T(8,128)}, f32[2,256,256]{2,1,0:T(8,128)}) custom-call(f32[32]{0:T(128)} %get-tuple-element.340.shift_ref, s32[1]{0:T(128)} %bitcast.34.index_ref, bf16[16,224,448]{2,1,0:T(8,128)(2,1)} %get-tuple-element.341.a_hbm, bf16[224,256]{1,0:T(8,128)(2,1)S(1)} %get-tuple-element.331.xlow_ref, f32[224,256]{1,0:T(8,128)S(1)} %get-tuple-element.330.x_ref), custom_call_target="tpu_custom_call" | custom-call | tf_op jit(solution)/shard_map/while/body/eval_jaxpr/sweep_product/pallas_call | solution.py:360
  1227.3 14.6 factor_and_apply.5
  1242.0 40.5 %sweep_product.5 = (f32[224,256]{1,0:T(8,128)}, f32[2,256,256]{2,1,0:T(8,128)}) custom-call(f32[32]{0:T(128)} %get-tuple-element.340.shift_ref, s32[1]{0:T(128)} %bitcast.34.index_ref, bf16[16,224,448]{2,1,0:T(8,128)(2,1)} %get-tuple-element.341.a_hbm, bf16[224,256]{1,0:T(8,128)(2,1)S(1)} %get-tuple-element.331.xlow_ref, f32[224,256]{1,0:T(8,128)S(1)} %get-tuple-element.330.x_ref), custom_call_target="tpu_custom_call" | custom-call | tf_op jit(solution)/shard_map/while/body/eval_jaxpr/sweep_product/pallas_call | solution.py:360
  1283.1 14.6 factor_and_apply.5
  1297.8 40.5 %sweep_product.5 = (f32[224,256]{1,0:T(8,128)}, f32[2,256,256]{2,1,0:T(8,128)}) custom-call(f32[32]{0:T(128)} %get-tuple-element.340.shift_ref, s32[1]{0:T(128)} %bitcast.34.index_ref, bf16[16,224,448]{2,1,0:T(8,128)(2,1)} %get-tuple-element.341.a_hbm, bf16[224,256]{1,0:T(8,128)(2,1)S(1)} %get-tuple-element.331.xlow_ref, f32[224,256]{1,0:T(8,128)S(1)} %get-tuple-element.330.x_ref), custom_call_target="tpu_custom_call" | custom-call | tf_op jit(solution)/shard_map/while/body/eval_jaxpr/sweep_product/pallas_call | solution.py:360
  1338.9 14.6 factor_and_apply.5
  1353.6 40.5 %sweep_product.5 = (f32[224,256]{1,0:T(8,128)}, f32[2,256,256]{2,1,0:T(8,128)}) custom-call(f32[32]{0:T(128)} %get-tuple-element.340.shift_ref, s32[1]{0:T(128)} %bitcast.34.index_ref, bf16[16,224,448]{2,1,0:T(8,128)(2,1)} %get-tuple-element.341.a_hbm, bf16[224,256]{1,0:T(8,128)(2,1)S(1)} %get-tuple-element.331.xlow_ref, f32[224,256]{1,0:T(8,128)S(1)} %get-tuple-element.330.x_ref), custom_call_target="tpu_custom_call" | custom-call | tf_op jit(solution)/shard_map/while/body/eval_jaxpr/sweep_product/pallas_call | solution.py:360
  1394.7 14.6 factor_and_apply.5
  1409.4 40.5 %sweep_product.5 = (f32[224,256]{1,0:T(8,128)}, f32[2,256,256]{2,1,0:T(8,128)}) custom-call(f32[32]{0:T(128)} %get-tuple-element.340.shift_ref, s32[1]{0:T(128)} %bitcast.34.index_ref, bf16[16,224,448]{2,1,0:T(8,128)(2,1)} %get-tuple-element.341.a_hbm, bf16[224,256]{1,0:T(8,128)(2,1)S(1)} %get-tuple-element.331.xlow_ref, f32[224,256]{1,0:T(8,128)S(1)} %get-tuple-element.330.x_ref), custom_call_target="tpu_custom_call" | custom-call | tf_op jit(solution)/shard_map/while/body/eval_jaxpr/sweep_product/pallas_call | solution.py:360
  1450.5 14.6 factor_and_apply.5
  1465.2 40.5 %sweep_product.5 = (f32[224,256]{1,0:T(8,128)}, f32[2,256,256]{2,1,0:T(8,128)}) custom-call(f32[32]{0:T(128)} %get-tuple-element.340.shift_ref, s32[1]{0:T(128)} %bitcast.34.index_ref, bf16[16,224,448]{2,1,0:T(8,128)(2,1)} %get-tuple-element.341.a_hbm, bf16[224,256]{1,0:T(8,128)(2,1)S(1)} %get-tuple-element.331.xlow_ref, f32[224,256]{1,0:T(8,128)S(1)} %get-tuple-element.330.x_ref), custom_call_target="tpu_custom_call" | custom-call | tf_op jit(solution)/shard_map/while/body/eval_jaxpr/sweep_product/pallas_call | solution.py:360
  1506.3 14.6 factor_and_apply.5
  1521.0 40.5 %sweep_product.5 = (f32[224,256]{1,0:T(8,128)}, f32[2,256,256]{2,1,0:T(8,128)}) custom-call(f32[32]{0:T(128)} %get-tuple-element.340.shift_ref, s32[1]{0:T(128)} %bitcast.34.index_ref, bf16[16,224,448]{2,1,0:T(8,128)(2,1)} %get-tuple-element.341.a_hbm, bf16[224,256]{1,0:T(8,128)(2,1)S(1)} %get-tuple-element.331.xlow_ref, f32[224,256]{1,0:T(8,128)S(1)} %get-tuple-element.330.x_ref), custom_call_target="tpu_custom_call" | custom-call | tf_op jit(solution)/shard_map/while/body/eval_jaxpr/sweep_product/pallas_call | solution.py:360
  1562.1 14.6 factor_and_apply.5
  1576.8 40.5 %sweep_product.5 = (f32[224,256]{1,0:T(8,128)}, f32[2,256,256]{2,1,0:T(8,128)}) custom-call(f32[32]{0:T(128)} %get-tuple-element.340.shift_ref, s32[1]{0:T(128)} %bitcast.34.index_ref, bf16[16,224,448]{2,1,0:T(8,128)(2,1)} %get-tuple-element.341.a_hbm, bf16[224,256]{1,0:T(8,128)(2,1)S(1)} %get-tuple-element.331.xlow_ref, f32[224,256]{1,0:T(8,128)S(1)} %get-tuple-element.330.x_ref), custom_call_target="tpu_custom_call" | custom-call | tf_op jit(solution)/shard_map/while/body/eval_jaxpr/sweep_product/pallas_call | solution.py:360
  1618.0 14.6 factor_and_apply.5
  1632.6 40.5 %sweep_product.5 = (f32[224,256]{1,0:T(8,128)}, f32[2,256,256]{2,1,0:T(8,128)}) custom-call(f32[32]{0:T(128)} %get-tuple-element.340.shift_ref, s32[1]{0:T(128)} %bitcast.34.index_ref, bf16[16,224,448]{2,1,0:T(8,128)(2,1)} %get-tuple-element.341.a_hbm, bf16[224,256]{1,0:T(8,128)(2,1)S(1)} %get-tuple-element.331.xlow_ref, f32[224,256]{1,0:T(8,128)S(1)} %get-tuple-element.330.x_ref), custom_call_target="tpu_custom_call" | custom-call | tf_op jit(solution)/shard_map/while/body/eval_jaxpr/sweep_product/pallas_call | solution.py:360
  1673.8 14.6 factor_and_apply.5
  1688.4 40.5 %sweep_product.5 = (f32[224,256]{1,0:T(8,128)}, f32[2,256,256]{2,1,0:T(8,128)}) custom-call(f32[32]{0:T(128)} %get-tuple-element.340.shift_ref, s32[1]{0:T(128)} %bitcast.34.index_ref, bf16[16,224,448]{2,1,0:T(8,128)(2,1)} %get-tuple-element.341.a_hbm, bf16[224,256]{1,0:T(8,128)(2,1)S(1)} %get-tuple-element.331.xlow_ref, f32[224,256]{1,0:T(8,128)S(1)} %get-tuple-element.330.x_ref), custom_call_target="tpu_custom_call" | custom-call | tf_op jit(solution)/shard_map/while/body/eval_jaxpr/sweep_product/pallas_call | solution.py:360
  1729.5 14.6 factor_and_apply.5
  1744.2 40.5 %sweep_product.5 = (f32[224,256]{1,0:T(8,128)}, f32[2,256,256]{2,1,0:T(8,128)}) custom-call(f32[32]{0:T(128)} %get-tuple-element.340.shift_ref, s32[1]{0:T(128)} %bitcast.34.index_ref, bf16[16,224,448]{2,1,0:T(8,128)(2,1)} %get-tuple-element.341.a_hbm, bf16[224,256]{1,0:T(8,128)(2,1)S(1)} %get-tuple-element.331.xlow_ref, f32[224,256]{1,0:T(8,128)S(1)} %get-tuple-element.330.x_ref), custom_call_target="tpu_custom_call" | custom-call | tf_op jit(solution)/shard_map/while/body/eval_jaxpr/sweep_product/pallas_call | solution.py:360
  1785.3 14.6 factor_and_apply.5
  1800.0 40.5 %sweep_product.5 = (f32[224,256]{1,0:T(8,128)}, f32[2,256,256]{2,1,0:T(8,128)}) custom-call(f32[32]{0:T(128)} %get-tuple-element.340.shift_ref, s32[1]{0:T(128)} %bitcast.34.index_ref, bf16[16,224,448]{2,1,0:T(8,128)(2,1)} %get-tuple-element.341.a_hbm, bf16[224,256]{1,0:T(8,128)(2,1)S(1)} %get-tuple-element.331.xlow_ref, f32[224,256]{1,0:T(8,128)S(1)} %get-tuple-element.330.x_ref), custom_call_target="tpu_custom_call" | custom-call | tf_op jit(solution)/shard_map/while/body/eval_jaxpr/sweep_product/pallas_call | solution.py:360
  1841.1 14.6 factor_and_apply.5
  1856.0 38.1 %final_product.1 = (f32[224,256]{1,0:T(8,128)}, f32[1,256,256]{2,1,0:T(8,128)S(1)}) custom-call(f32[32]{0:T(128)} %get-tuple-element.371, s32[1]{0:T(128)} %constant.57.clone.1.index_ref, bf16[16,224,448]{2,1,0:T(8,128)(2,1)} %get-tuple-element.352, bf16[224,256]{1,0:T(8,128)(2,1)S(1)} %get-tuple-element.208.xlow_ref, f32[224,256]{1,0:T(8,128)S(1)} %get-tuple-element.209.x_ref), custom_call_target="tpu_custom_call" | custom-call | tf_op jit(solution)/shard_map/final_product/pallas_call | solution.py:360
  (112 shorter events, 91.5 us)
Async XLA Ops:
  8.8 43.9 %all-to-all-start = ((bf16[8,224,896]{2,1,0:T(8,128)(2,1)}), bf16[8,224,896]{2,1,0:T(8,128)(2,1)S(1)}, u32[]{:S(2)}, u32[]{:S(2)}) async-start(bf16[8,224,896]{2,1,0:T(8,128)(2,1)} %bitcast.49), calls=%async_computation | async-start | bytes 6422528 | tf_op jit(solution)/shard_map/all_to_all | solution.py:408
  69.0 42.1 %copy-start.3 = (f32[8,128]{1,0:T(8,128)S(1)}, f32[8,128]{1,0:T(8,128)}, u32[]{:S(2)}) copy-start(f32[8,128]{1,0:T(8,128)} %get-tuple-element.332) | copy-start | bytes 12292 | tf_op jit(solution)/shard_map/while
  126.3 40.4 %copy-start.3 = (f32[8,128]{1,0:T(8,128)S(1)}, f32[8,128]{1,0:T(8,128)}, u32[]{:S(2)}) copy-start(f32[8,128]{1,0:T(8,128)} %get-tuple-element.332) | copy-start | bytes 12292 | tf_op jit(solution)/shard_map/while
  182.0 40.3 %copy-start.3 = (f32[8,128]{1,0:T(8,128)S(1)}, f32[8,128]{1,0:T(8,128)}, u32[]{:S(2)}) copy-start(f32[8,128]{1,0:T(8,128)} %get-tuple-element.332) | copy-start | bytes 12292 | tf_op jit(solution)/shard_map/while
  237.6 40.5 %copy-start.3 = (f32[8,128]{1,0:T(8,128)S(1)}, f32[8,128]{1,0:T(8,128)}, u32[]{:S(2)}) copy-start(f32[8,128]{1,0:T(8,128)} %get-tuple-element.332) | copy-start | bytes 12292 | tf_op jit(solution)/shard_map/while
  293.4 40.5 %copy-start.3 = (f32[8,128]{1,0:T(8,128)S(1)}, f32[8,128]{1,0:T(8,128)}, u32[]{:S(2)}) copy-start(f32[8,128]{1,0:T(8,128)} %get-tuple-element.332) | copy-start | bytes 12292 | tf_op jit(solution)/shard_map/while
  349.2 40.5 %copy-start.3 = (f32[8,128]{1,0:T(8,128)S(1)}, f32[8,128]{1,0:T(8,128)}, u32[]{:S(2)}) copy-start(f32[8,128]{1,0:T(8,128)} %get-tuple-element.332) | copy-start | bytes 12292 | tf_op jit(solution)/shard_map/while
  405.0 40.6 %copy-start.3 = (f32[8,128]{1,0:T(8,128)S(1)}, f32[8,128]{1,0:T(8,128)}, u32[]{:S(2)}) copy-start(f32[8,128]{1,0:T(8,128)} %get-tuple-element.332) | copy-start | bytes 12292 | tf_op jit(solution)/shard_map/while
  460.8 40.5 %copy-start.3 = (f32[8,128]{1,0:T(8,128)S(1)}, f32[8,128]{1,0:T(8,128)}, u32[]{:S(2)}) copy-start(f32[8,128]{1,0:T(8,128)} %get-tuple-element.332) | copy-start | bytes 12292 | tf_op jit(solution)/shard_map/while
  516.6 40.5 %copy-start.3 = (f32[8,128]{1,0:T(8,128)S(1)}, f32[8,128]{1,0:T(8,128)}, u32[]{:S(2)}) copy-start(f32[8,128]{1,0:T(8,128)} %get-tuple-element.332) | copy-start | bytes 12292 | tf_op jit(solution)/shard_map/while
  572.4 40.5 %copy-start.3 = (f32[8,128]{1,0:T(8,128)S(1)}, f32[8,128]{1,0:T(8,128)}, u32[]{:S(2)}) copy-start(f32[8,128]{1,0:T(8,128)} %get-tuple-element.332) | copy-start | bytes 12292 | tf_op jit(solution)/shard_map/while
  628.2 40.5 %copy-start.3 = (f32[8,128]{1,0:T(8,128)S(1)}, f32[8,128]{1,0:T(8,128)}, u32[]{:S(2)}) copy-start(f32[8,128]{1,0:T(8,128)} %get-tuple-element.332) | copy-start | bytes 12292 | tf_op jit(solution)/shard_map/while
  684.0 40.5 %copy-start.3 = (f32[8,128]{1,0:T(8,128)S(1)}, f32[8,128]{1,0:T(8,128)}, u32[]{:S(2)}) copy-start(f32[8,128]{1,0:T(8,128)} %get-tuple-element.332) | copy-start | bytes 12292 | tf_op jit(solution)/shard_map/while
  739.8 40.5 %copy-start.3 = (f32[8,128]{1,0:T(8,128)S(1)}, f32[8,128]{1,0:T(8,128)}, u32[]{:S(2)}) copy-start(f32[8,128]{1,0:T(8,128)} %get-tuple-element.332) | copy-start | bytes 12292 | tf_op jit(solution)/shard_map/while
  795.5 40.5 %copy-start.3 = (f32[8,128]{1,0:T(8,128)S(1)}, f32[8,128]{1,0:T(8,128)}, u32[]{:S(2)}) copy-start(f32[8,128]{1,0:T(8,128)} %get-tuple-element.332) | copy-start | bytes 12292 | tf_op jit(solution)/shard_map/while
  851.4 40.5 %copy-start.3 = (f32[8,128]{1,0:T(8,128)S(1)}, f32[8,128]{1,0:T(8,128)}, u32[]{:S(2)}) copy-start(f32[8,128]{1,0:T(8,128)} %get-tuple-element.332) | copy-start | bytes 12292 | tf_op jit(solution)/shard_map/while
  907.2 40.5 %copy-start.3 = (f32[8,128]{1,0:T(8,128)S(1)}, f32[8,128]{1,0:T(8,128)}, u32[]{:S(2)}) copy-start(f32[8,128]{1,0:T(8,128)} %get-tuple-element.332) | copy-start | bytes 12292 | tf_op jit(solution)/shard_map/while
  963.0 40.5 %copy-start.3 = (f32[8,128]{1,0:T(8,128)S(1)}, f32[8,128]{1,0:T(8,128)}, u32[]{:S(2)}) copy-start(f32[8,128]{1,0:T(8,128)} %get-tuple-element.332) | copy-start | bytes 12292 | tf_op jit(solution)/shard_map/while
  1018.8 40.5 %copy-start.3 = (f32[8,128]{1,0:T(8,128)S(1)}, f32[8,128]{1,0:T(8,128)}, u32[]{:S(2)}) copy-start(f32[8,128]{1,0:T(8,128)} %get-tuple-element.332) | copy-start | bytes 12292 | tf_op jit(solution)/shard_map/while
  1074.6 40.5 %copy-start.3 = (f32[8,128]{1,0:T(8,128)S(1)}, f32[8,128]{1,0:T(8,128)}, u32[]{:S(2)}) copy-start(f32[8,128]{1,0:T(8,128)} %get-tuple-element.332) | copy-start | bytes 12292 | tf_op jit(solution)/shard_map/while
  1130.4 40.5 %copy-start.3 = (f32[8,128]{1,0:T(8,128)S(1)}, f32[8,128]{1,0:T(8,128)}, u32[]{:S(2)}) copy-start(f32[8,128]{1,0:T(8,128)} %get-tuple-element.332) | copy-start | bytes 12292 | tf_op jit(solution)/shard_map/while
  1186.2 40.5 %copy-start.3 = (f32[8,128]{1,0:T(8,128)S(1)}, f32[8,128]{1,0:T(8,128)}, u32[]{:S(2)}) copy-start(f32[8,128]{1,0:T(8,128)} %get-tuple-element.332) | copy-start | bytes 12292 | tf_op jit(solution)/shard_map/while
  1242.0 40.5 %copy-start.3 = (f32[8,128]{1,0:T(8,128)S(1)}, f32[8,128]{1,0:T(8,128)}, u32[]{:S(2)}) copy-start(f32[8,128]{1,0:T(8,128)} %get-tuple-element.332) | copy-start | bytes 12292 | tf_op jit(solution)/shard_map/while
  1297.8 40.5 %copy-start.3 = (f32[8,128]{1,0:T(8,128)S(1)}, f32[8,128]{1,0:T(8,128)}, u32[]{:S(2)}) copy-start(f32[8,128]{1,0:T(8,128)} %get-tuple-element.332) | copy-start | bytes 12292 | tf_op jit(solution)/shard_map/while
  1353.6 40.5 %copy-start.3 = (f32[8,128]{1,0:T(8,128)S(1)}, f32[8,128]{1,0:T(8,128)}, u32[]{:S(2)}) copy-start(f32[8,128]{1,0:T(8,128)} %get-tuple-element.332) | copy-start | bytes 12292 | tf_op jit(solution)/shard_map/while
  1409.4 40.5 %copy-start.3 = (f32[8,128]{1,0:T(8,128)S(1)}, f32[8,128]{1,0:T(8,128)}, u32[]{:S(2)}) copy-start(f32[8,128]{1,0:T(8,128)} %get-tuple-element.332) | copy-start | bytes 12292 | tf_op jit(solution)/shard_map/while
  1465.2 40.5 %copy-start.3 = (f32[8,128]{1,0:T(8,128)S(1)}, f32[8,128]{1,0:T(8,128)}, u32[]{:S(2)}) copy-start(f32[8,128]{1,0:T(8,128)} %get-tuple-element.332) | copy-start | bytes 12292 | tf_op jit(solution)/shard_map/while
  1521.0 40.5 %copy-start.3 = (f32[8,128]{1,0:T(8,128)S(1)}, f32[8,128]{1,0:T(8,128)}, u32[]{:S(2)}) copy-start(f32[8,128]{1,0:T(8,128)} %get-tuple-element.332) | copy-start | bytes 12292 | tf_op jit(solution)/shard_map/while
  1576.8 40.5 %copy-start.3 = (f32[8,128]{1,0:T(8,128)S(1)}, f32[8,128]{1,0:T(8,128)}, u32[]{:S(2)}) copy-start(f32[8,128]{1,0:T(8,128)} %get-tuple-element.332) | copy-start | bytes 12292 | tf_op jit(solution)/shard_map/while
  1632.6 40.5 %copy-start.3 = (f32[8,128]{1,0:T(8,128)S(1)}, f32[8,128]{1,0:T(8,128)}, u32[]{:S(2)}) copy-start(f32[8,128]{1,0:T(8,128)} %get-tuple-element.332) | copy-start | bytes 12292 | tf_op jit(solution)/shard_map/while
  1688.4 40.5 %copy-start.3 = (f32[8,128]{1,0:T(8,128)S(1)}, f32[8,128]{1,0:T(8,128)}, u32[]{:S(2)}) copy-start(f32[8,128]{1,0:T(8,128)} %get-tuple-element.332) | copy-start | bytes 12292 | tf_op jit(solution)/shard_map/while
  1744.2 40.5 %copy-start.3 = (f32[8,128]{1,0:T(8,128)S(1)}, f32[8,128]{1,0:T(8,128)}, u32[]{:S(2)}) copy-start(f32[8,128]{1,0:T(8,128)} %get-tuple-element.332) | copy-start | bytes 12292 | tf_op jit(solution)/shard_map/while
  1800.0 40.5 %copy-start.3 = (f32[8,128]{1,0:T(8,128)S(1)}, f32[8,128]{1,0:T(8,128)}, u32[]{:S(2)}) copy-start(f32[8,128]{1,0:T(8,128)} %get-tuple-element.332) | copy-start | bytes 12292 | tf_op jit(solution)/shard_map/while
  1856.0 39.9 %copy-start.2 = (f32[224,256]{1,0:T(8,128)}, f32[224,256]{1,0:T(8,128)S(1)}, u32[]{:S(2)}) copy-start(f32[224,256]{1,0:T(8,128)S(1)} %get-tuple-element.209.x_ref) | copy-start | bytes 688132

commit v2 on v0

v2 whole, which is shorter than its diff:
```python
import functools

import jax
import jax.numpy as jnp
from jax import lax
from jax.experimental import pallas as pl
from jax.experimental.pallas import tpu as pltpu
from jax.sharding import PartitionSpec as P

HI = lax.Precision.HIGHEST
ROW_CONTRACT = (((0,), (0,)), ((), ()))
GRID_AXES = ("row", "col")
NB = 32
FIRST_ERR = 1e-2
SECOND_ERR = 1.6e-7
LINE = (0, 1, -1, 2)
MESH_ID = pl.DeviceIdType.MESH


def factor_panel(panel, start, nb):
    width = panel.shape[1]
    tiles = width // 128
    groups = nb // 8
    p = [[panel[8*v:8*v+8, 128*t:128*t+128] for t in range(tiles)] for v in range(groups)]
    sub = lax.broadcasted_iota(jnp.int32, (8, 128), 0)
    lane = lax.broadcasted_iota(jnp.int32, (8, 128), 1)
    dinv = [None]*groups
    for g in range(groups):
        cols = [start + 8*g + j for j in range(8)]
        b = [[jnp.broadcast_to(p[v][c//128][:, c%128:c%128+1], (8, 128)) for v in range(g, groups)] for c in cols]
        dg = jnp.ones((8, 128), jnp.float32)
        for j in range(8):
            c = cols[j]
            tc = c // 128
            d = jnp.broadcast_to(b[j][0][j:j+1, :], (8, 128))
            inv = 1.0 / d
            dg = jnp.where(sub == j, inv, dg)
            m = [b[j][v]*inv for v in range(groups-g)]
            for q in range(j+1, 8):
                f = jnp.broadcast_to(b[q][0][j:j+1, :], (8, 128))
                b[q] = [b[q][v] - m[v]*f for v in range(groups-g)]
            m[0] = jnp.where(sub > j, m[0], 0.0)
            for t in range(tiles):
                r = jnp.broadcast_to(p[g][t][j:j+1, :], (8, 128))
                if t == tc:
                    r = jnp.where(lane == c % 128, 1.0, r)
                for v in range(g, groups):
                    old = p[v][t]
                    if t == tc:
                        old = jnp.where(lane == c % 128, jnp.where(sub == j, 1.0, 0.0) if v == g else 0.0, old)
                    p[v][t] = old - m[v-g]*r
            for v in range(g):
                p[v][tc] = jnp.where(lane == c % 128, 0.0, p[v][tc])
        dinv[g] = dg
    rows = []
    for v in range(groups):
        s = jnp.sqrt(dinv[v])
        rows.append(jnp.concatenate([p[v][t]*s for t in range(tiles)], axis=1))
    return jnp.concatenate(rows, axis=0)


def chol_inverse(w_ref, hooks={}, nb=NB):
    size = w_ref.shape[0]
    for k in range(size // nb):
        lo, hi = k*nb, (k+1)*nb
        panel = factor_panel(w_ref[lo:hi, :], lo, nb)
        w_ref[lo:hi, :] = panel
        if k in hooks:
            hooks[k]()
        if hi < size:
            upd = lax.dot_general(panel, panel, (((0,), (0,)), ((), ())), precision=HI, preferred_element_type=jnp.float32)
            upd = upd[hi:, :]
            lane = lax.broadcasted_iota(jnp.int32, (size-hi, size), 1)
            old = w_ref[hi:, :]
            old = jnp.where((lane >= lo) & (lane < hi), 0.0, old)
            w_ref[hi:, :] = old - upd


def lower_mask(x):
    r = lax.broadcasted_iota(jnp.int32, x.shape, 0)
    c = lax.broadcasted_iota(jnp.int32, x.shape, 1)
    return jnp.where(r >= c, x, 0.0)


def cholesky_inverse_kernel(g_ref, o_ref, work):
    work[...] = g_ref[...]
    chol_inverse(work)
    o_ref[...] = lower_mask(work[...])


def cholesky_inverse(gram):
    return pl.pallas_call(
        cholesky_inverse_kernel,
        out_shape=jax.ShapeDtypeStruct(gram.shape, jnp.float32),
        in_specs=[pl.BlockSpec(memory_space=pltpu.VMEM)],
        out_specs=pl.BlockSpec(memory_space=pltpu.VMEM),
        scratch_shapes=[pltpu.VMEM(gram.shape, jnp.float32)],
    )(gram)


def apply_inverse(y_loc, factor_inv):
    return lax.dot_general(y_loc, factor_inv, (((1,), (1,)), ((), ())), precision=HI, preferred_element_type=jnp.float32)


def orthonormalize(y_loc, total_rows):
    y_low = y_loc.astype(jnp.bfloat16)
    gram_one = lax.psum(lax.dot_general(y_low, y_low, ROW_CONTRACT, preferred_element_type=jnp.float32), GRID_AXES) / total_rows
    y_mid = apply_inverse(y_loc, cholesky_inverse(gram_one))
    gram_two = lax.psum(lax.dot_general(y_mid, y_mid, ROW_CONTRACT, precision=HI, preferred_element_type=jnp.float32), GRID_AXES) / total_rows
    return apply_inverse(y_mid, cholesky_inverse(gram_two))

def lower_half(err):
    r = lax.broadcasted_iota(jnp.int32, err.shape, 0)
    c = lax.broadcasted_iota(jnp.int32, err.shape, 1)
    return jnp.where(r > c, err, jnp.where(r == c, 0.5 * err, 0.0))


def eye(size):
    return jnp.where(lax.broadcasted_iota(jnp.int32, (size, size), 0) == lax.broadcasted_iota(jnp.int32, (size, size), 1), 1.0, 0.0)


def mul(a, b):
    return jnp.dot(a, b, precision=HI, preferred_element_type=jnp.float32)


def mul_t(a, b):
    return lax.dot_general(a, b, (((1,), (1,)), ((), ())), precision=HI, preferred_element_type=jnp.float32)


def subspace_kernel(dims, total_rows, shift_ref, a_hbm, start_ref, x_ref, h_ref, flag_ref,
                    a_buf, xlow, xbuf, acc, gloc, rhalf, ghalf, slots, red, gsum, work,
                    a_sem, send_near, recv_near, send_far, recv_far, send_line, recv_line, send_end, recv_end,
                    send_core, recv_core, send_half, recv_half, send_rs, recv_rs, send_bc, recv_bc, send_out, recv_out):
    rows_y, cols, rows = dims
    chips_x = cols // 2
    half = rows // 2
    row, col = lax.axis_index("row"), lax.axis_index("col")
    chip, core = lax.div(col, 2), lax.rem(col, 2)
    size = x_ref.shape[1]
    lanes = size // 2
    part = size // 2
    strip = part // (rows_y * chips_x)

    def place(dx, dy):
        return lax.rem(chip + dx + chips_x, chips_x), lax.rem(row + dy + rows_y, rows_y)

    def device(dx, dy, flip=False):
        px, py = place(dx, dy)
        return {"row": py, "col": px * 2 + ((1 - core) if flip else core)}

    def slot(dx, dy):
        px, py = place(dx, dy)
        return py * chips_x + px

    def axis_pair(h, u, v):
        return (u, v) if h == 0 else (v, u)

    plane = [(dx, dy) for dy in LINE for dx in LINE if (dx, dy) != (0, 0)]
    barrier = pltpu.get_barrier_semaphore()
    for dx, dy in plane:
        pl.semaphore_signal(barrier, inc=1, device_id=device(dx, dy), device_id_type=MESH_ID)
    pl.semaphore_signal(barrier, inc=1, device_id=device(0, 0, True), device_id_type=MESH_ID)
    pl.semaphore_wait(barrier, len(plane) + 1)

    load = pltpu.make_async_copy(a_hbm, a_buf, a_sem)
    load.start()

    def gather_product():
        sent = []

        def send(src, dst, ssem, rsem, dev):
            copy = pltpu.make_async_remote_copy(src_ref=src, dst_ref=dst, send_sem=ssem, recv_sem=rsem, device_id=dev, device_id_type=MESH_ID)
            copy.start()
            sent.append(copy)
            return copy

        base = pl.multiple_of(core * rows, 32)

        def unit(h, dx, dy, lane=None):
            where = pl.ds(pl.multiple_of(base + h * half, 16), half)
            if lane is None:
                return xbuf.at[slot(dx, dy), where, :]
            return xbuf.at[slot(dx, dy), where, pl.ds(lane * lanes, lanes)]

        def own(h):
            return xlow.at[pl.ds(h * half, half), :]

        near, far, line, end, cross = {}, {}, {}, {}, {}

        def start_near(h, d):
            near[h, d] = send(own(h), unit(h, 0, 0), send_near.at[h, (d + 1) // 2], recv_near.at[h, (d + 1) // 2], device(*axis_pair(h, d, 0)))

        def start_far(h, d):
            piece = unit(h, *axis_pair(h, -d, 0), lane=(d + 1) // 2)
            far[h, d] = send(piece, piece, send_far.at[h, (d + 1) // 2], recv_far.at[h, (d + 1) // 2], device(*axis_pair(h, d, 0)))

        def start_line(h, u):
            for d in (1, -1):
                piece = unit(h, *axis_pair(h, u, 0))
                line[h, u, d] = send(own(h) if u == 0 else piece, piece, send_line.at[h, u + 1, (d + 1) // 2], recv_line.at[h, u + 1, (d + 1) // 2],
                                     device(*axis_pair(h, 0, d)))

        def start_end(h, u, d):
            piece = unit(h, *axis_pair(h, u, -d), lane=(d + 1) // 2)
            end[h, u, d] = send(piece, piece, send_end.at[h, u + 1, (d + 1) // 2], recv_end.at[h, u + 1, (d + 1) // 2], device(*axis_pair(h, 0, d)))

        def start_cross(dx, dy):
            block = xbuf.at[slot(dx, dy), pl.ds(base, rows), :]
            index = (dy + 1) * 4 + dx + 1
            cross[dx, dy] = send(xlow if (dx, dy) == (0, 0) else block, block, send_core.at[index], recv_core.at[index], device(0, 0, True))

        def product(dx, dy, first=False):
            cross[dx, dy].wait_recv()
            term = jnp.dot(a_buf[slot(dx, dy)], xbuf[slot(dx, dy)], preferred_element_type=jnp.float32)
            acc[...] = term if first else acc[...] + term

        for d in (1, -1):
            for h in (0, 1):
                start_near(h, d)
        for h in (0, 1):
            start_line(h, 0)
        start_cross(0, 0)
        xbuf[slot(0, 0), pl.ds(base, rows), :] = xlow[...]
        for d in (1, -1):
            for h in (0, 1):
                near[h, d].wait_recv()
                start_far(h, d)
                start_line(h, -d)
        for d in (1, -1):
            for h in (0, 1):
                line[h, 0, d].wait_recv()
                start_end(h, 0, d)
        for d in (1, -1):
            start_cross(d, 0)
            start_cross(0, d)
        product(0, 0, first=True)
        for h in (0, 1):
            for d in (1, -1):
                far[h, d].wait_recv()
            start_line(h, 2)
        for u in (1, -1):
            for d in (1, -1):
                for h in (0, 1):
                    line[h, u, d].wait_recv()
                    start_end(h, u, d)
        for u in (1, -1):
            for d in (1, -1):
                start_cross(u, d)
        for d in (1, -1):
            product(d, 0)
            product(0, d)
        for h in (0, 1):
            for d in (1, -1):
                end[h, 0, d].wait_recv()
        start_cross(2, 0)
        start_cross(0, 2)
        for d in (1, -1):
            for h in (0, 1):
                line[h, 2, d].wait_recv()
                start_end(h, 2, d)
        for u in (1, -1):
            for d in (1, -1):
                product(u, d)
        for u in (1, -1):
            for h in (0, 1):
                for d in (1, -1):
                    end[h, u, d].wait_recv()
        for u in (1, -1):
            start_cross(2, u)
            start_cross(u, 2)
        product(2, 0)
        product(0, 2)
        for h in (0, 1):
            for d in (1, -1):
                end[h, 2, d].wait_recv()
        start_cross(2, 2)
        for u in (1, -1):
            product(2, u)
            product(u, 2)
        product(2, 2)

        for copy in sent:
            copy.wait_send()

    kept = pl.ds(pl.multiple_of(core * part, 8), part)
    given = pl.ds(pl.multiple_of((1 - core) * part, 8), part)
    mine = slot(0, 0)
    mine_rows = pl.ds(pl.multiple_of(core * part + mine * strip, 8), strip)

    def send(src, dst, ssem, rsem, dev):
        copy = pltpu.make_async_remote_copy(src_ref=src, dst_ref=dst, send_sem=ssem, recv_sem=rsem, device_id=dev, device_id_type=MESH_ID)
        copy.start()
        return copy

    class GroupSum:
        def __init__(self, n):
            self.n = n
            self.sent = []
            self.waits = [send(gloc.at[n, given, :], rhalf.at[n], send_half.at[n], recv_half.at[n], device(0, 0, True))]

        def arrive(self):
            for copy in self.waits:
                copy.wait_recv()
            self.sent += self.waits
            self.waits = []

        def scatter(self):
            n = self.n
            self.arrive()
            ghalf[n] = gloc[n, kept, :] + rhalf[n]
            for i, (dx, dy) in enumerate(plane):
                rows_of = pl.ds(pl.multiple_of(slot(dx, dy) * strip, 8), strip)
                self.waits.append(send(ghalf.at[n, rows_of, :], slots.at[n, mine], send_rs.at[n, i], recv_rs.at[n, i], device(dx, dy)))
            slots[n, mine] = ghalf[n, pl.ds(pl.multiple_of(mine * strip, 8), strip), :]

        def spread(self):
            n = self.n
            self.arrive()
            red[n] = jnp.sum(slots[n], axis=0)
            for i, (dx, dy) in enumerate(plane):
                self.waits.append(send(red.at[n], gsum.at[n, mine_rows, :], send_bc.at[n, i], recv_bc.at[n, i], device(dx, dy)))
            gsum[n, mine_rows, :] = red[n]

        def cross(self):
            n = self.n
            self.arrive()
            self.waits.append(send(gsum.at[n, kept, :], gsum.at[n, kept, :], send_out.at[n], recv_out.at[n], device(0, 0, True)))

        def finish(self):
            for copy in self.sent:
                copy.wait_send()

    scale = 1.0 / total_rows
    unit_mat = eye(size)

    def sweep(t):
        gather_product()
        y_val = acc[...] - shift_ref[t] * x_ref[...]
        y_low = y_val.astype(jnp.bfloat16)
        gloc[0] = lax.dot_general(y_low, y_low, ROW_CONTRACT, preferred_element_type=jnp.float32)
        one = GroupSum(0)
        acc[...] = y_val
        gloc[1] = lax.dot_general(y_val, y_val, ROW_CONTRACT, precision=HI, preferred_element_type=jnp.float32)
        two = GroupSum(1)
        one.scatter()
        two.scatter()
        one.spread()
        two.spread()
        one.cross()
        one.arrive()
        work[...] = gsum[0] * scale
        chol_inverse(work, {1: two.cross})
        two.arrive()
        first = lower_mask(work[...])
        gram_two = mul_t(mul(first, gsum[1] * scale), first)
        err = gram_two - unit_mat
        far_one = jnp.where(jnp.sum(err * err, axis=(0, 1), keepdims=True) <= FIRST_ERR, 0.0, 1.0)
        second = unit_mat - lower_half(err)
        err = mul_t(mul(second, gram_two), second) - unit_mat
        far_two = jnp.where(jnp.sum(err * err, axis=(0, 1), keepdims=True) <= SECOND_ERR, 0.0, 1.0)
        flag_ref[...] = jnp.maximum(flag_ref[...], jnp.maximum(far_one, far_two))
        second = second - mul(lower_half(err), second)
        x_val = mul_t(acc[...], mul(second, first))
        xlow[...] = x_val.astype(jnp.bfloat16)
        x_ref[...] = x_val
        one.finish()
        two.finish()

    flag_ref[...] = jnp.zeros_like(flag_ref)
    x_ref[...] = start_ref[...]
    xlow[...] = start_ref[...].astype(jnp.bfloat16)
    load.wait()

    @pl.loop(0, shift_ref.shape[0])
    def _(t):
        sweep(t)

    gather_product()
    gloc[0] = lax.dot_general(x_ref[...], acc[...], ROW_CONTRACT, precision=HI, preferred_element_type=jnp.float32)
    total = GroupSum(0)
    total.scatter()
    total.spread()
    total.cross()
    total.arrive()
    h_ref[...] = gsum[0] / total_rows
    total.finish()


def iterate(dims, total_rows, shifts, a_blocks, x_start):
    rows_y, cols, rows = dims
    size = x_start.shape[1]
    chips = rows_y * cols // 2
    dma = pltpu.SemaphoreType.DMA
    vmem = pl.BlockSpec(memory_space=pltpu.VMEM)
    peers = chips - 1
    strip = size // 2 // chips
    return pl.pallas_call(
        functools.partial(subspace_kernel, dims, total_rows),
        out_shape=(
            jax.ShapeDtypeStruct((rows, size), jnp.float32),
            jax.ShapeDtypeStruct((size, size), jnp.float32),
            jax.ShapeDtypeStruct((8, 128), jnp.float32),
        ),
        in_specs=[pl.BlockSpec(memory_space=pltpu.SMEM), pl.BlockSpec(memory_space=pl.ANY), vmem],
        out_specs=(vmem,) * 3,
        scratch_shapes=[
            pltpu.VMEM(a_blocks.shape, jnp.bfloat16),
            pltpu.VMEM((rows, size), jnp.bfloat16),
            pltpu.VMEM((chips, 2 * rows, size), jnp.bfloat16),
            pltpu.VMEM((rows, size), jnp.float32),
            pltpu.VMEM((2, size, size), jnp.float32),
            pltpu.VMEM((2, size // 2, size), jnp.float32),
            pltpu.VMEM((2, size // 2, size), jnp.float32),
            pltpu.VMEM((2, chips, strip, size), jnp.float32),
            pltpu.VMEM((2, strip, size), jnp.float32),
            pltpu.VMEM((2, size, size), jnp.float32),
            pltpu.VMEM((size, size), jnp.float32),
            dma,
            dma((2, 2)), dma((2, 2)), dma((2, 2)), dma((2, 2)),
            dma((2, 4, 2)), dma((2, 4, 2)), dma((2, 4, 2)), dma((2, 4, 2)),
            dma((16,)), dma((16,)), dma((2,)), dma((2,)),
            dma((2, peers)), dma((2, peers)), dma((2, peers)), dma((2, peers)), dma((2,)), dma((2,)),
        ],
        compiler_params=pltpu.CompilerParams(collective_id=0, has_side_effects=True, vmem_limit_bytes=56 * 2**20),
        name="subspace_sweeps",
    )(shifts, a_blocks, x_start)


def solution(mesh):
    row_count = mesh.shape["row"]
    col_count = mesh.shape["col"]

    def apply_operator(a_rows, x_loc):
        x_full = lax.all_gather(x_loc.astype(jnp.bfloat16), GRID_AXES, axis=0, tiled=True)
        return jnp.dot(a_rows, x_full, preferred_element_type=jnp.float32)

    def careful_program(a_rows, x_loc, shift_vec, total_rows):
        def sweep(sweep_idx, x_cur):
            applied = apply_operator(a_rows, x_cur)
            return orthonormalize(applied - shift_vec[sweep_idx] * x_cur, total_rows)

        x_loc = lax.fori_loop(0, shift_vec.shape[0], sweep, x_loc)
        applied = apply_operator(a_rows, x_loc)
        local_part = lax.dot_general(x_loc, applied, ROW_CONTRACT, precision=HI, preferred_element_type=jnp.float32)
        return x_loc, lax.psum(local_part, GRID_AXES) / total_rows

    def local_program(a_blk, x_start, shift_vec):
        total_rows = a_blk.shape[0] * row_count
        rows = x_start.shape[0]
        dims = (row_count, col_count, rows)
        a_rows = lax.all_to_all(a_blk, "col", split_axis=0, concat_axis=1, tiled=True)
        a_blocks = a_rows.reshape(rows, row_count * col_count // 2, 2 * rows).transpose(1, 0, 2)

        x_loc, rayleigh, flag = iterate(dims, total_rows, shift_vec, a_blocks, x_start)
        return lax.cond(
            flag[0, 0] > 0.0,
            lambda: careful_program(a_rows, x_start, shift_vec, total_rows),
            lambda: (x_loc, rayleigh),
        )

    return jax.shard_map(
        local_program,
        mesh=mesh,
        in_specs=(P(("batch", "row"), "col"), P(("batch", "row", "col"), None), P("batch")),
        out_specs=(P(("batch", "row", "col"), None), P("batch", None)),
        check_vma=False,
    )
```

time: 13500 us -> 1560 us (0.12)
  waiting for transfers between devices: 7260 us -> 0 us
  other arithmetic: 4150 us -> 0 us
  Pallas kernels: 0 us -> 1470 us
  local copies, waits for them, and re-layouts: 804 us -> 20.7 us
  matrix products: 583 us -> 0 us
  blocking collectives: 458 us -> 44.2 us
    psum x65 -> x0, waiting for transfers between devices: 6100 us -> none  [the longest x32 3060 us: orthonormalize(): lax.psum(lax.dot_general(y_low, y_low, ROW_CONTRACT, preferred_element_ty...]
    another operation x576 -> x0, other arithmetic: 3910 us -> none  [the longest x224 1230 us: orthonormalize(): chol_two = jnp.linalg.cholesky(gram_two)]
    pallas_call x0 -> x1, Pallas kernels: none -> 1470 us  [iterate(): pl.pallas_call(functools.partial(subspace_kernel, dims, total_rows), out_...]
    reduce_scatter x32 -> x0, waiting for transfers between devices: 931 us -> none  [apply_operator(): lax.psum_scatter(partial_rows, 'col', scatter_dimension=0, tiled=True)]
    another operation x577 -> x0, local copies, waits for them, and re-layouts: 620 us -> none  [the longest x257 308 us: orthonormalize(): lax.linalg.triangular_solve(chol_one, y_loc, left_side=False, lower=True,...]
    all_gather x33 -> x0, blocking collectives: 458 us -> none  [apply_operator(): x_column = lax.all_gather(x_moved, 'row', axis=0, tiled=True)]
    another operation x320 -> x0, matrix products: 430 us -> none  [the longest x64 109 us: orthonormalize(): chol_two = jnp.linalg.cholesky(gram_two)]
    ppermute x33 -> x0, waiting for transfers between devices: 196 us -> none  [apply_operator(): x_moved = lax.ppermute(x_low, GRID_AXES, perm_pairs)]
  transfers between devices with their start and end apart: 131 -> 0, of which waited for: 131 -> 0; matrix products, arithmetic and copies ran while one was open for 0% -> 0% of each run, Pallas kernels for 0% -> 0%
where the time goes in v2:
time: 1560 us; the launch traced here: 1550 us
  Pallas kernels  1470 us (94%)
  blocking collectives  44.2 us (3%)
  local copies, waits for them, and re-layouts  20.7 us (1%)
    pallas_call x1, Pallas kernels, iterate(): pl.pallas_call(functools.partial(subspace_kernel, dims, total_rows), out_...  1470 us
    all_to_all x1, blocking collectives, local_program(): lax.all_to_all(a_blk, 'col', split_axis=0, concat_axis=1, tiled=True)  44.2 us

profile of v2, /device:TPU:97, one launch (start us, length us, event | category | flops | bytes accessed | tf_op | source)
XLA Modules:
  0.0 1546.8 jit_solution(17291900546849186272)
XLA Ops:
  7.2 1.6 copy.33.start_ref
  8.8 44.2 %all_to_all.19 = bf16[8,224,896]{2,1,0:T(8,128)(2,1)S(1)} all-to-all(bf16[8,224,896]{2,1,0:T(8,128)(2,1)} %bitcast.44), channel_id=1, replica_groups=mesh['batch'=1,'row'=4,'col'=8] {'col'}, dimensions={0} | all-to-all | bytes 6422528 | tf_op jit(solution)/shard_map/all_to_all | solution.py:451
  53.0 2.7 copy.9
  55.7 6.9 reshape.15
  62.6 0.0 copy-start.2
  62.6 5.9 copy.14
  68.5 0.0 copy-done.2
  68.5 1466.9 %subspace_sweeps.1 = (f32[224,256]{1,0:T(8,128)}, f32[256,256]{1,0:T(8,128)S(1)}, f32[8,128]{1,0:T(8,128)}) custom-call(f32[32]{0:T(128)S(1)} %copy-done.2, bf16[16,224,448]{2,1,0:T(8,128)(2,1)} %bitcast.43, f32[224,256]{1,0:T(8,128)} %copy.33.start_ref), custom_call_target="tpu_custom_call" | custom-call | tf_op jit(solution)/shard_map/subspace_sweeps/pallas_call | solution.py:397
  1535.4 1.2 slice.3
  1537.3 1.6 copy.34
  1538.9 0.7 copy.35
  (1 shorter events, 0.0 us)
Async XLA Ops:
  62.6 5.9 copy-start.2

commit v3 on v2

v3 whole, which is shorter than its diff:
```python
import functools

import jax
import jax.numpy as jnp
from jax import lax
from jax.experimental import pallas as pl
from jax.experimental.pallas import tpu as pltpu
from jax.sharding import PartitionSpec as P

HI = lax.Precision.HIGHEST
ROW_CONTRACT = (((0,), (0,)), ((), ()))
GRID_AXES = ("row", "col")
NB = 32
GRP = 16
FIRST_ERR = 1e-2
SECOND_ERR = 1.6e-7
LINE = (0, 1, -1, 2)
STRAIGHT = (0, 2)
MESH_ID = pl.DeviceIdType.MESH


def factor_panel(panel, other, offset):
    nb = panel.shape[0]
    parts = nb // 8
    p = [panel[8*v:8*v+8, :] for v in range(parts)]
    o = [other[8*v:8*v+8, :] for v in range(parts)]
    sub = lax.broadcasted_iota(jnp.int32, (8, 128), 0)
    lane = lax.broadcasted_iota(jnp.int32, (8, 128), 1)
    scales = [jnp.ones((8, 128), jnp.float32)] * parts
    for first in range(0, nb, GRP):
        b = [{v: jnp.broadcast_to(p[v][:, offset+first+q:offset+first+q+1], (8, 128)) for v in range((first+q)//8, parts)} for q in range(GRP)]
        for q in range(GRP):
            g, j, c = (first + q) // 8, (first + q) % 8, offset + first + q
            inv = 1.0 / jnp.broadcast_to(b[q][g][j:j+1, :], (8, 128))
            scales[g] = jnp.where(sub == j, inv, scales[g])
            m = {v: b[q][v] * inv for v in range(g, parts)}
            for z in range(q+1, GRP):
                gz, jz = (first + z) // 8, (first + z) % 8
                f = jnp.broadcast_to(b[q][gz][jz:jz+1, :], (8, 128))
                for v in range(gz, parts):
                    b[z][v] = b[z][v] - m[v] * f
            m[g] = jnp.where(sub > j, m[g], 0.0)
            row = jnp.where(lane == c, 1.0, jnp.broadcast_to(p[g][j:j+1, :], (8, 128)))
            row_o = jnp.broadcast_to(o[g][j:j+1, :], (8, 128))
            for v in range(parts):
                old = jnp.where(lane == c, jnp.where(sub == j, 1.0, 0.0) if v == g else 0.0, p[v])
                p[v] = old - m[v] * row if v >= g else old
                if v >= g:
                    o[v] = o[v] - m[v] * row_o
    scales = [jnp.sqrt(s) for s in scales]
    return (jnp.concatenate([p[v] * scales[v] for v in range(parts)], axis=0),
            jnp.concatenate([o[v] * scales[v] for v in range(parts)], axis=0))


def chol_inverse(w_ref):
    size = w_ref.shape[0]
    half = size // 2

    @pl.loop(0, 2)
    def _(t):
        here = pl.ds(pl.multiple_of(t * half, half), half)
        there = pl.ds(pl.multiple_of((1 - t) * half, half), half)
        lane = lax.broadcasted_iota(jnp.int32, (NB, half), 1)
        for lo in range(0, half, NB):
            rows = pl.ds(pl.multiple_of(t * half + lo, NB), NB)
            p, o = w_ref[rows, here], w_ref[rows, there]
            p, o = factor_panel(p, o, lo)
            w_ref[rows, here] = p
            w_ref[rows, there] = o
            if lo + NB < half:
                rest = pl.ds(pl.multiple_of(t * half + lo + NB, NB), half - lo - NB)
                lanes = lax.broadcasted_iota(jnp.int32, (half - lo - NB, half), 1)
                u = p[:, lo + NB:]
                old = jnp.where((lanes >= lo) & (lanes < lo + NB), 0.0, w_ref[rest, here])
                w_ref[rest, here] = old - lax.dot_general(u, p, ROW_CONTRACT, precision=HI, preferred_element_type=jnp.float32)
                w_ref[rest, there] = w_ref[rest, there] - lax.dot_general(u, o, ROW_CONTRACT, precision=HI, preferred_element_type=jnp.float32)

        @pl.when(t == 0)
        def _():
            u = w_ref[:half, half:]
            w_ref[half:, half:] = w_ref[half:, half:] - lax.dot_general(u, u, ROW_CONTRACT, precision=HI, preferred_element_type=jnp.float32)
            done = lower_mask(w_ref[:half, :half])
            w_ref[half:, :half] = -lax.dot_general(u, done, ROW_CONTRACT, precision=HI, preferred_element_type=jnp.float32)


def lower_mask(x):
    r = lax.broadcasted_iota(jnp.int32, x.shape, 0)
    c = lax.broadcasted_iota(jnp.int32, x.shape, 1)
    return jnp.where(r >= c, x, 0.0)


def cholesky_inverse_kernel(g_ref, o_ref, work):
    work[...] = g_ref[...]
    chol_inverse(work)
    o_ref[...] = lower_mask(work[...])


def cholesky_inverse(gram):
    return pl.pallas_call(
        cholesky_inverse_kernel,
        out_shape=jax.ShapeDtypeStruct(gram.shape, jnp.float32),
        in_specs=[pl.BlockSpec(memory_space=pltpu.VMEM)],
        out_specs=pl.BlockSpec(memory_space=pltpu.VMEM),
        scratch_shapes=[pltpu.VMEM(gram.shape, jnp.float32)],
    )(gram)


def apply_inverse(y_loc, factor_inv):
    return lax.dot_general(y_loc, factor_inv, (((1,), (1,)), ((), ())), precision=HI, preferred_element_type=jnp.float32)


def orthonormalize(y_loc, total_rows):
    y_low = y_loc.astype(jnp.bfloat16)
    gram_one = lax.psum(lax.dot_general(y_low, y_low, ROW_CONTRACT, preferred_element_type=jnp.float32), GRID_AXES) / total_rows
    y_mid = apply_inverse(y_loc, cholesky_inverse(gram_one))
    gram_two = lax.psum(lax.dot_general(y_mid, y_mid, ROW_CONTRACT, precision=HI, preferred_element_type=jnp.float32), GRID_AXES) / total_rows
    return apply_inverse(y_mid, cholesky_inverse(gram_two))

def lower_half(err):
    r = lax.broadcasted_iota(jnp.int32, err.shape, 0)
    c = lax.broadcasted_iota(jnp.int32, err.shape, 1)
    return jnp.where(r > c, err, jnp.where(r == c, 0.5 * err, 0.0))


def eye(size):
    return jnp.where(lax.broadcasted_iota(jnp.int32, (size, size), 0) == lax.broadcasted_iota(jnp.int32, (size, size), 1), 1.0, 0.0)


def mul(a, b):
    return jnp.dot(a, b, precision=HI, preferred_element_type=jnp.float32)


def mul_t(a, b):
    return lax.dot_general(a, b, (((1,), (1,)), ((), ())), precision=HI, preferred_element_type=jnp.float32)


def subspace_kernel(dims, total_rows, shift_ref, a_hbm, start_ref, x_ref, h_ref, flag_ref,
                    a_buf, xlow, xbuf, acc, gloc, slots, red, gsum, work,
                    a_sem, send_near, recv_near, send_far, recv_far, send_line, recv_line, send_end, recv_end,
                    send_core, recv_core, send_rs, recv_rs, send_bc, recv_bc):
    rows_y, cols, rows = dims
    chips_x = cols // 2
    half = rows // 2
    row, col = lax.axis_index("row"), lax.axis_index("col")
    chip, core = lax.div(col, 2), lax.rem(col, 2)
    size = x_ref.shape[1]
    lanes = size // 2
    strip = size // (rows_y * cols)

    def place(dx, dy):
        return lax.rem(chip + dx + chips_x, chips_x), lax.rem(row + dy + rows_y, rows_y)

    def device(dx, dy, flip=False):
        px, py = place(dx, dy)
        return {"row": py, "col": px * 2 + ((1 - core) if flip else core)}

    def slot(dx, dy):
        px, py = place(dx, dy)
        return py * chips_x + px

    def axis_pair(h, u, v):
        return (u, v) if h == 0 else (v, u)

    peers = [(dx, dy, flip) for dx in LINE for dy in LINE for flip in (False, True) if (dx, dy, flip) != (0, 0, False)]
    peers.sort(key=lambda peer: -(2 * abs(peer[0]) + 2 * abs(peer[1]) + peer[2]))
    barrier = pltpu.get_barrier_semaphore()
    for peer in peers:
        pl.semaphore_signal(barrier, inc=1, device_id=device(*peer), device_id_type=MESH_ID)
    pl.semaphore_wait(barrier, len(peers))

    load = pltpu.make_async_copy(a_hbm, a_buf, a_sem)
    load.start()

    def gather_product():
        sent = []

        def send(src, dst, ssem, rsem, dev):
            copy = pltpu.make_async_remote_copy(src_ref=src, dst_ref=dst, send_sem=ssem, recv_sem=rsem, device_id=dev, device_id_type=MESH_ID)
            copy.start()
            sent.append(copy)
            return copy

        base = pl.multiple_of(core * rows, 32)

        def unit(h, dx, dy, lane=None):
            where = pl.ds(pl.multiple_of(base + h * half, 16), half)
            if lane is None:
                return xbuf.at[slot(dx, dy), where, :]
            return xbuf.at[slot(dx, dy), where, pl.ds(lane * lanes, lanes)]

        def own(h):
            return xlow.at[pl.ds(h * half, half), :]

        near, far, line, end, cross = {}, {}, {}, {}, {}
        signs = (1, -1)

        def start_near(h, d):
            near[h, d] = send(own(h), unit(h, 0, 0), send_near.at[h, (d + 1) // 2], recv_near.at[h, (d + 1) // 2], device(*axis_pair(h, d, 0)))

        def start_far(h):
            far[h] = send(own(h), unit(h, 0, 0), send_far.at[h], recv_far.at[h], device(*axis_pair(h, 2, 0)))

        def start_line(h, u):
            piece = unit(h, *axis_pair(h, u, 0))
            source = own(h) if u == 0 else piece
            for d in signs:
                line[h, u, d] = send(source, piece, send_line.at[h, u + 1, (d + 1) // 2], recv_line.at[h, u + 1, (d + 1) // 2],
                                     device(*axis_pair(h, 0, d)))
            if u in STRAIGHT:
                end[h, u, 1] = send(source, piece, send_end.at[h, u + 1, 0], recv_end.at[h, u + 1, 0], device(*axis_pair(h, 0, 2)))

        def start_end(h, u, d):
            piece = unit(h, *axis_pair(h, u, -d), lane=(d + 1) // 2)
            end[h, u, d] = send(piece, piece, send_end.at[h, u + 1, (d + 1) // 2], recv_end.at[h, u + 1, (d + 1) // 2], device(*axis_pair(h, 0, d)))

        def start_cross(h, dx, dy):
            piece = unit(h, dx, dy)
            index = (dy + 1) * 4 + dx + 1
            cross[h, dx, dy] = send(own(h) if (dx, dy) == (0, 0) else piece, piece, send_core.at[h, index], recv_core.at[h, index], device(0, 0, True))

        def product(dx, dy, first=False):
            for h in (0, 1):
                cross[h, dx, dy].wait_recv()
            term = jnp.dot(a_buf[slot(dx, dy)], xbuf[slot(dx, dy)], preferred_element_type=jnp.float32)
            acc[...] = term if first else acc[...] + term

        def got_line(us):
            for u in us:
                for d in signs:
                    for h in (0, 1):
                        line[h, u, d].wait_recv()
                        if u not in STRAIGHT:
                            start_end(h, u, d)
                        start_cross(h, *axis_pair(h, u, -d))

        def got_end(us):
            for u in us:
                for h in (0, 1):
                    for d in signs:
                        if (h, u, d) in end:
                            end[h, u, d].wait_recv()
                    start_cross(h, *axis_pair(h, u, 2))

        def got_far():
            for h in (0, 1):
                far[h].wait_recv()
                start_line(h, 2)
                start_cross(h, *axis_pair(h, 2, 0))

        for d in signs:
            for h in (0, 1):
                start_near(h, d)
        for h in (0, 1):
            start_far(h)
        for h in (0, 1):
            start_line(h, 0)
            start_cross(h, 0, 0)
        xbuf[slot(0, 0), pl.ds(base, rows), :] = xlow[...]
        for d in signs:
            for h in (0, 1):
                near[h, d].wait_recv()
                start_line(h, -d)
                start_cross(h, *axis_pair(h, -d, 0))
        got_far()
        got_line((0,))
        product(0, 0, first=True)
        got_line((1, -1))
        for d in signs:
            product(d, 0)
            product(0, d)
        got_end((0,))
        got_line((2,))
        product(2, 0)
        product(0, 2)
        for u in signs:
            for d in signs:
                product(u, d)
        got_end((1, -1))
        got_end((2,))
        for u in signs:
            product(2, u)
            product(u, 2)
        product(2, 2)

        for copy in sent:
            copy.wait_send()

    def strip_of(dx, dy, flip):
        px, py = place(dx, dy)
        return py * cols + px * 2 + ((1 - core) if flip else core)

    def strip_rows(index):
        return pl.ds(pl.multiple_of(index * strip, 8), strip)

    mine = strip_of(0, 0, False)

    def send(src, dst, ssem, rsem, dev):
        copy = pltpu.make_async_remote_copy(src_ref=src, dst_ref=dst, send_sem=ssem, recv_sem=rsem, device_id=dev, device_id_type=MESH_ID)
        copy.start()
        return copy

    class GroupSum:
        def __init__(self, n):
            self.n = n
            self.sent = []
            self.waits = [send(gloc.at[n, strip_rows(strip_of(*peer)), :], slots.at[n, mine], send_rs.at[n, i], recv_rs.at[n, i], device(*peer))
                          for i, peer in enumerate(peers)]
            slots[n, mine] = gloc[n, strip_rows(mine), :]

        def arrive(self):
            for copy in self.waits:
                copy.wait_recv()
            self.sent += self.waits
            self.waits = []

        def spread(self):
            n = self.n
            self.arrive()
            red[n] = jnp.sum(slots[n], axis=0)
            self.waits = [send(red.at[n], gsum.at[n, strip_rows(mine), :], send_bc.at[n, i], recv_bc.at[n, i], device(*peer))
                          for i, peer in enumerate(peers)]
            gsum[n, strip_rows(mine), :] = red[n]

        def finish(self):
            for copy in self.sent:
                copy.wait_send()

    scale = 1.0 / total_rows
    unit_mat = eye(size)

    def sweep(t):
        gather_product()
        y_val = acc[...] - shift_ref[t] * x_ref[...]
        y_low = y_val.astype(jnp.bfloat16)
        gloc[0] = lax.dot_general(y_low, y_low, ROW_CONTRACT, preferred_element_type=jnp.float32)
        one = GroupSum(0)
        acc[...] = y_val
        gloc[1] = lax.dot_general(y_val, y_val, ROW_CONTRACT, precision=HI, preferred_element_type=jnp.float32)
        two = GroupSum(1)
        one.spread()
        two.spread()
        one.arrive()
        work[...] = gsum[0] * scale
        chol_inverse(work)
        two.arrive()
        first = lower_mask(work[...])
        gram_two = mul_t(mul(first, gsum[1] * scale), first)
        err = gram_two - unit_mat
        far_one = jnp.where(jnp.sum(err * err, axis=(0, 1), keepdims=True) <= FIRST_ERR, 0.0, 1.0)
        second = unit_mat - lower_half(err)
        near_x = mul_t(acc[...], mul(second, first))
        err = mul_t(mul(second, gram_two), second) - unit_mat
        far_two = jnp.where(jnp.sum(err * err, axis=(0, 1), keepdims=True) <= SECOND_ERR, 0.0, 1.0)
        flag_ref[...] = jnp.maximum(flag_ref[...], jnp.maximum(far_one, far_two))
        x_val = near_x - mul_t(near_x, lower_half(err))
        xlow[...] = x_val.astype(jnp.bfloat16)
        x_ref[...] = x_val
        one.finish()
        two.finish()

    flag_ref[...] = jnp.zeros_like(flag_ref)
    x_ref[...] = start_ref[...]
    xlow[...] = start_ref[...].astype(jnp.bfloat16)
    load.wait()

    @pl.loop(0, shift_ref.shape[0])
    def _(t):
        sweep(t)

    gather_product()
    gloc[0] = lax.dot_general(x_ref[...], acc[...], ROW_CONTRACT, precision=HI, preferred_element_type=jnp.float32)
    total = GroupSum(0)
    total.spread()
    total.arrive()
    h_ref[...] = gsum[0] / total_rows
    total.finish()


def iterate(dims, total_rows, shifts, a_blocks, x_start):
    rows_y, cols, rows = dims
    size = x_start.shape[1]
    chips = rows_y * cols // 2
    dma = pltpu.SemaphoreType.DMA
    vmem = pl.BlockSpec(memory_space=pltpu.VMEM)
    peers = 2 * chips - 1
    strip = size // (2 * chips)
    return pl.pallas_call(
        functools.partial(subspace_kernel, dims, total_rows),
        out_shape=(
            jax.ShapeDtypeStruct((rows, size), jnp.float32),
            jax.ShapeDtypeStruct((size, size), jnp.float32),
            jax.ShapeDtypeStruct((8, 128), jnp.float32),
        ),
        in_specs=[pl.BlockSpec(memory_space=pltpu.SMEM), pl.BlockSpec(memory_space=pl.ANY), vmem],
        out_specs=(vmem,) * 3,
        scratch_shapes=[
            pltpu.VMEM(a_blocks.shape, jnp.bfloat16),
            pltpu.VMEM((rows, size), jnp.bfloat16),
            pltpu.VMEM((chips, 2 * rows, size), jnp.bfloat16),
            pltpu.VMEM((rows, size), jnp.float32),
            pltpu.VMEM((2, size, size), jnp.float32),
            pltpu.VMEM((2, 2 * chips, strip, size), jnp.float32),
            pltpu.VMEM((2, strip, size), jnp.float32),
            pltpu.VMEM((2, size, size), jnp.float32),
            pltpu.VMEM((size, size), jnp.float32),
            dma,
            dma((2, 2)), dma((2, 2)), dma((2,)), dma((2,)),
            dma((2, 4, 2)), dma((2, 4, 2)), dma((2, 4, 2)), dma((2, 4, 2)),
            dma((2, 16)), dma((2, 16)),
            dma((2, peers)), dma((2, peers)), dma((2, peers)), dma((2, peers)),
        ],
        compiler_params=pltpu.CompilerParams(collective_id=0, has_side_effects=True, vmem_limit_bytes=56 * 2**20),
        name="subspace_sweeps",
    )(shifts, a_blocks, x_start)


def solution(mesh):
    row_count = mesh.shape["row"]
    col_count = mesh.shape["col"]

    def apply_operator(a_rows, x_loc):
        x_full = lax.all_gather(x_loc.astype(jnp.bfloat16), GRID_AXES, axis=0, tiled=True)
        return jnp.dot(a_rows, x_full, preferred_element_type=jnp.float32)

    def careful_program(a_rows, x_loc, shift_vec, total_rows):
        def sweep(sweep_idx, x_cur):
            applied = apply_operator(a_rows, x_cur)
            return orthonormalize(applied - shift_vec[sweep_idx] * x_cur, total_rows)

        x_loc = lax.fori_loop(0, shift_vec.shape[0], sweep, x_loc)
        applied = apply_operator(a_rows, x_loc)
        local_part = lax.dot_general(x_loc, applied, ROW_CONTRACT, precision=HI, preferred_element_type=jnp.float32)
        return x_loc, lax.psum(local_part, GRID_AXES) / total_rows

    def local_program(a_blk, x_start, shift_vec):
        total_rows = a_blk.shape[0] * row_count
        rows = x_start.shape[0]
        dims = (row_count, col_count, rows)
        a_rows = lax.all_to_all(a_blk, "col", split_axis=0, concat_axis=1, tiled=True)
        a_blocks = a_rows.reshape(rows, row_count * col_count // 2, 2 * rows).transpose(1, 0, 2)

        x_loc, rayleigh, flag = iterate(dims, total_rows, shift_vec, a_blocks, x_start)
        return lax.cond(
            flag[0, 0] > 0.0,
            lambda: careful_program(a_rows, x_start, shift_vec, total_rows),
            lambda: (x_loc, rayleigh),
        )

    return jax.shard_map(
        local_program,
        mesh=mesh,
        in_specs=(P(("batch", "row"), "col"), P(("batch", "row", "col"), None), P("batch")),
        out_specs=(P(("batch", "row", "col"), None), P("batch", None)),
        check_vma=False,
    )
```

time: 1560 us -> 1410 us (0.904)
  Pallas kernels: 1470 us -> 1330 us
    pallas_call x1, Pallas kernels: 1470 us -> 1330 us  [iterate(): pl.pallas_call(functools.partial(subspace_kernel, dims, total_rows), out_...]
where the time goes in v3:
time: 1410 us
  Pallas kernels  1330 us (94%)
  blocking collectives  44.2 us (3%)
  local copies, waits for them, and re-layouts  20.7 us (1%)
  between operations  14.7 us (1%)
    pallas_call x1, Pallas kernels, iterate(): pl.pallas_call(functools.partial(subspace_kernel, dims, total_rows), out_...  1330 us
    all_to_all x1, blocking collectives, local_program(): lax.all_to_all(a_blk, 'col', split_axis=0, concat_axis=1, tiled=True)  44.2 us

profile of v3, /device:TPU:97, one launch (start us, length us, event | category | flops | bytes accessed | tf_op | source)
XLA Modules:
  0.0 1407.1 jit_solution(11177967501989349743)
XLA Ops:
  7.2 1.6 copy.33.start_ref
  8.8 44.2 %all_to_all.19 = bf16[8,224,896]{2,1,0:T(8,128)(2,1)S(1)} all-to-all(bf16[8,224,896]{2,1,0:T(8,128)(2,1)} %bitcast.44), channel_id=1, replica_groups=mesh['batch'=1,'row'=4,'col'=8] {'col'}, dimensions={0} | all-to-all | bytes 6422528 | tf_op jit(solution)/shard_map/all_to_all | solution.py:439
  53.0 2.7 copy.9
  55.7 6.9 reshape.15
  62.6 0.0 copy-start.2
  62.6 5.9 copy.14
  68.5 0.0 copy-done.2
  68.5 1327.5 %subspace_sweeps.1 = (f32[224,256]{1,0:T(8,128)}, f32[256,256]{1,0:T(8,128)S(1)}, f32[8,128]{1,0:T(8,128)}) custom-call(f32[32]{0:T(128)S(1)} %copy-done.2, bf16[16,224,448]{2,1,0:T(8,128)(2,1)} %bitcast.43, f32[224,256]{1,0:T(8,128)} %copy.33.start_ref), custom_call_target="tpu_custom_call" | custom-call | tf_op jit(solution)/shard_map/subspace_sweeps/pallas_call | solution.py:387
  1396.1 1.2 slice.3
  1397.9 1.6 copy.34
  1399.6 0.7 copy.35
  (1 shorter events, 0.0 us)
Async XLA Ops:
  62.6 5.9 copy-start.2

commit v4 on v3

--- a/solution.py
+++ b/solution.py
@@ -109,12 +109,21 @@
     return lax.dot_general(y_loc, factor_inv, (((1,), (1,)), ((), ())), precision=HI, preferred_element_type=jnp.float32)
 
 
-def orthonormalize(y_loc, total_rows):
-    y_low = y_loc.astype(jnp.bfloat16)
-    gram_one = lax.psum(lax.dot_general(y_low, y_low, ROW_CONTRACT, preferred_element_type=jnp.float32), GRID_AXES) / total_rows
-    y_mid = apply_inverse(y_loc, cholesky_inverse(gram_one))
-    gram_two = lax.psum(lax.dot_general(y_mid, y_mid, ROW_CONTRACT, precision=HI, preferred_element_type=jnp.float32), GRID_AXES) / total_rows
-    return apply_inverse(y_mid, cholesky_inverse(gram_two))
+def group_sum(part, devices):
+    strips = lax.all_to_all(part.reshape(devices, part.shape[0] // devices, part.shape[1]), GRID_AXES, split_axis=0, concat_axis=0)
+    return lax.all_gather(jnp.sum(strips, axis=0), GRID_AXES, axis=0, tiled=True)
+
+
+def orthonormalize(y_loc, total_rows, devices):
+    def one_pass(which, y_cur):
+        y_low = y_cur.astype(jnp.bfloat16)
+        gram_low = lax.dot_general(y_low, y_low, ROW_CONTRACT, preferred_element_type=jnp.float32)
+        gram_full = lax.dot_general(y_cur, y_cur, ROW_CONTRACT, precision=HI, preferred_element_type=jnp.float32)
+        gram = group_sum(jnp.where(which == 0, gram_low, gram_full), devices) / total_rows
+        return apply_inverse(y_cur, cholesky_inverse(gram))
+
+    return lax.fori_loop(0, 2, one_pass, y_loc)
+
 
 def lower_half(err):
     r = lax.broadcasted_iota(jnp.int32, err.shape, 0)
@@ -183,10 +192,10 @@
         base = pl.multiple_of(core * rows, 32)
 
         def unit(h, dx, dy, lane=None):
-            where = pl.ds(pl.multiple_of(base + h * half, 16), half)
+            where = pl.ds(pl.multiple_of(slot(dx, dy) * (2 * rows) + base + h * half, 16), half)
             if lane is None:
-                return xbuf.at[slot(dx, dy), where, :]
-            return xbuf.at[slot(dx, dy), where, pl.ds(lane * lanes, lanes)]
+                return xbuf.at[where, :]
+            return xbuf.at[where, pl.ds(lane * lanes, lanes)]
 
         def own(h):
             return xlow.at[pl.ds(h * half, half), :]
@@ -218,10 +227,13 @@
             index = (dy + 1) * 4 + dx + 1
             cross[h, dx, dy] = send(own(h) if (dx, dy) == (0, 0) else piece, piece, send_core.at[h, index], recv_core.at[h, index], device(0, 0, True))
 
-        def product(dx, dy, first=False):
-            for h in (0, 1):
-                cross[h, dx, dy].wait_recv()
-            term = jnp.dot(a_buf[slot(dx, dy)], xbuf[slot(dx, dy)], preferred_element_type=jnp.float32)
+        def product(others, dy, first=False):
+            for dx in ((2,) if others else (0, 1, -1)):
+                for h in (0, 1):
+                    cross[h, dx, dy].wait_recv()
+            pair = lax.div(slot(2 if others else 0, dy), 2)
+            block = xbuf[pl.ds(pl.multiple_of(pair * (4 * rows), 32), 4 * rows), :]
+            term = jnp.dot(a_buf[pair], block, preferred_element_type=jnp.float32)
             acc[...] = term if first else acc[...] + term
 
         def got_line(us):
@@ -255,7 +267,7 @@
         for h in (0, 1):
             start_line(h, 0)
             start_cross(h, 0, 0)
-        xbuf[slot(0, 0), pl.ds(base, rows), :] = xlow[...]
+        xbuf[pl.ds(pl.multiple_of(slot(0, 0) * (2 * rows) + base, 32), rows), :] = xlow[...]
         for d in signs:
             for h in (0, 1):
                 near[h, d].wait_recv()
@@ -263,25 +275,19 @@
                 start_cross(h, *axis_pair(h, -d, 0))
         got_far()
         got_line((0,))
-        product(0, 0, first=True)
         got_line((1, -1))
-        for d in signs:
-            product(d, 0)
-            product(0, d)
+        product(False, 0, first=True)
         got_end((0,))
         got_line((2,))
-        product(2, 0)
-        product(0, 2)
+        product(True, 0)
         for u in signs:
-            for d in signs:
-                product(u, d)
+            product(False, u)
         got_end((1, -1))
         got_end((2,))
         for u in signs:
-            product(2, u)
-            product(u, 2)
-        product(2, 2)
-
+            product(True, u)
+        product(False, 2)
+        product(True, 2)
         for copy in sent:
             copy.wait_send()
 
@@ -396,7 +402,7 @@
         scratch_shapes=[
             pltpu.VMEM(a_blocks.shape, jnp.bfloat16),
             pltpu.VMEM((rows, size), jnp.bfloat16),
-            pltpu.VMEM((chips, 2 * rows, size), jnp.bfloat16),
+            pltpu.VMEM((chips * 2 * rows, size), jnp.bfloat16),
             pltpu.VMEM((rows, size), jnp.float32),
             pltpu.VMEM((2, size, size), jnp.float32),
             pltpu.VMEM((2, 2 * chips, strip, size), jnp.float32),
@@ -419,30 +425,38 @@
     col_count = mesh.shape["col"]
 
     def apply_operator(a_rows, x_loc):
-        x_full = lax.all_gather(x_loc.astype(jnp.bfloat16), GRID_AXES, axis=0, tiled=True)
+        rows, size = x_loc.shape
+        x_parts = x_loc.astype(jnp.bfloat16).reshape(rows, 4, size // 4).transpose(1, 0, 2)
+        gathered = lax.map(lambda part: lax.all_gather(part, GRID_AXES, axis=0, tiled=True), x_parts)
+        x_full = gathered.transpose(1, 0, 2).reshape(gathered.shape[1], size)
         return jnp.dot(a_rows, x_full, preferred_element_type=jnp.float32)
 
-    def careful_program(a_rows, x_loc, shift_vec, total_rows):
-        def sweep(sweep_idx, x_cur):
+    def careful_program(a_blocks, x_loc, shift_vec, total_rows):
+        a_rows = a_blocks.transpose(1, 0, 2).reshape(x_loc.shape[0], total_rows)
+
+        sweeps = shift_vec.shape[0]
+
+        def sweep(sweep_idx, carry):
+            x_cur, _ = carry
             applied = apply_operator(a_rows, x_cur)
-            return orthonormalize(applied - shift_vec[sweep_idx] * x_cur, total_rows)
-
-        x_loc = lax.fori_loop(0, shift_vec.shape[0], sweep, x_loc)
-        applied = apply_operator(a_rows, x_loc)
+            shift = shift_vec[jnp.minimum(sweep_idx, sweeps - 1)]
+            x_next = orthonormalize(applied - shift * x_cur, total_rows, row_count * col_count)
+            return jnp.where(sweep_idx < sweeps, x_next, x_cur), applied
+
+        x_loc, applied = lax.fori_loop(0, sweeps + 1, sweep, (x_loc, x_loc))
         local_part = lax.dot_general(x_loc, applied, ROW_CONTRACT, precision=HI, preferred_element_type=jnp.float32)
-        return x_loc, lax.psum(local_part, GRID_AXES) / total_rows
+        return x_loc, group_sum(local_part, row_count * col_count) / total_rows
 
     def local_program(a_blk, x_start, shift_vec):
         total_rows = a_blk.shape[0] * row_count
         rows = x_start.shape[0]
         dims = (row_count, col_count, rows)
-        a_rows = lax.all_to_all(a_blk, "col", split_axis=0, concat_axis=1, tiled=True)
-        a_blocks = a_rows.reshape(rows, row_count * col_count // 2, 2 * rows).transpose(1, 0, 2)
+        a_blocks = lax.all_to_all(a_blk.reshape(col_count, rows, a_blk.shape[1]), "col", split_axis=0, concat_axis=0)
 
         x_loc, rayleigh, flag = iterate(dims, total_rows, shift_vec, a_blocks, x_start)
         return lax.cond(
             flag[0, 0] > 0.0,
-            lambda: careful_program(a_rows, x_start, shift_vec, total_rows),
+            lambda: careful_program(a_blocks, x_start, shift_vec, total_rows),
             lambda: (x_loc, rayleigh),
         )
 

time: 1410 us -> 1390 us (0.986)
  local copies, waits for them, and re-layouts: 20.7 us -> 4.48 us
    pallas_call x1, Pallas kernels: 1330 us -> 1340 us  [iterate(): pl.pallas_call(functools.partial(subspace_kernel, dims, total_rows), out_...]
where the time goes in v4:
time: 1390 us
  Pallas kernels  1340 us (96%)
  blocking collectives  44.2 us (3%)
    pallas_call x1, Pallas kernels, iterate(): pl.pallas_call(functools.partial(subspace_kernel, dims, total_rows), out_...  1340 us
    all_to_all x1, blocking collectives, local_program(): lax.all_to_all(a_blk.reshape(col_count, rows, a_blk.shape[1]), 'col', spl...  44.2 us

profile of v4, /device:TPU:97, one launch (start us, length us, event | category | flops | bytes accessed | tf_op | source)
XLA Modules:
  0.0 1393.7 jit_solution(10242554961179570293)
XLA Ops:
  0.6 0.0 copy-start
  0.6 0.9 copy.56.start_ref
  1.6 44.2 %all_to_all.19.a_hbm = bf16[8,224,896]{2,1,0:T(8,128)(2,1)S(1)} all-to-all(bf16[8,224,896]{2,1,0:T(8,128)(2,1)} %bitcast.55), channel_id=1, replica_groups=mesh['batch'=1,'row'=4,'col'=8] {'col'}, dimensions={0} | all-to-all | bytes 6422528 | tf_op jit(solution)/shard_map/all_to_all | solution.py:454
  45.8 0.0 copy-done
  45.8 1343.4 %subspace_sweeps.1 = (f32[224,256]{1,0:T(8,128)}, f32[256,256]{1,0:T(8,128)S(1)}, f32[8,128]{1,0:T(8,128)}) custom-call(f32[32]{0:T(128)S(1)} %copy-done, bf16[8,224,896]{2,1,0:T(8,128)(2,1)S(1)} %all_to_all.19.a_hbm, f32[224,256]{1,0:T(8,128)S(1)} %copy.56.start_ref), custom_call_target="tpu_custom_call" | custom-call | tf_op jit(solution)/shard_map/subspace_sweeps/pallas_call | solution.py:393
  1389.2 1.2 slice.3
  1391.0 0.3 conditional.1
  1391.3 1.6 copy.59
  1393.0 0.7 copy.60
Async XLA Ops:
  0.6 45.1 %copy-start = (f32[32]{0:T(128)S(1)}, f32[32]{0:T(128)}, u32[]{:S(2)}) copy-start(f32[32]{0:T(128)} %shift_ref.1) | copy-start | bytes 388
